TPU v7x, 256 devices: a whole 4x4x8 slice. The times are simulated.
256 devices in a mesh: dp: 8 (over z_lo, y), expert: 32 (over x, z_hi, core).
Axes of the slice: x: 4, y: 4, z: 8 (z_hi: 4, z_lo: 2; z = z_hi * 2 + z_lo), core: 2. Of those that a mesh axis runs over, the one named last changes fastest.
Arguments:
- tokens: bfloat16 [32768, 2048], P(('dp', 'expert')), may hold values from -6 to 6
- out_grad: bfloat16 [32768, 2048], P(('dp', 'expert')), may hold values from -6 to 6
- expert_ids: int32 [32768, 2], P(('dp', 'expert')), may hold values from 0 to 31, all different within a row; in each aligned block of 128 rows (0 to 127, 128 to 255, ...) at most 16 rows name the same one
- gate_probs: float32 [32768, 2], P(('dp', 'expert')), may hold values from 0.1 to 1
- held_expert: int32 [32], replicated, may hold values from 0 to 31, each once
- swap_pairs: int32 [4], replicated, may hold values from 0 to 15, as said below
- w_in: bfloat16 [32, 2048, 1536], P('expert', 'dp'), may hold values from -0.125 to 0.125
- w_down: bfloat16 [32, 2048, 768], P('expert', 'dp'), may hold values from -0.21875 to 0.21875
- m_in: bfloat16 [32, 2048, 1536], P('expert', 'dp'), may hold values from -12 to 12
- m_down: bfloat16 [32, 2048, 768], P('expert', 'dp'), may hold values from -12 to 12
- v_in: bfloat16 [32, 2048, 1536], P('expert', 'dp'), may hold values from 4 to 400
- v_down: bfloat16 [32, 2048, 768], P('expert', 'dp'), may hold values from 4 to 400
Outputs:
- token_grad: bfloat16 [32768, 2048], P(('dp', 'expert'))
- prob_grad: float32 [32768, 2], P(('dp', 'expert'))
- new_w_in: bfloat16 [32, 2048, 1536], P('expert', 'dp')
- new_w_down: bfloat16 [32, 2048, 768], P('expert', 'dp')
- new_m_in: bfloat16 [32, 2048, 1536], P('expert', 'dp')
- new_m_down: bfloat16 [32, 2048, 768], P('expert', 'dp')
- new_v_in: bfloat16 [32, 2048, 1536], P('expert', 'dp')
- new_v_down: bfloat16 [32, 2048, 768], P('expert', 'dp')
Inputs may be any that keep to these rules, and one draw needn't show every extreme that they name: `expert_ids`: each row names 2 different experts; among the 128 rows of one device no expert is named by more than 16 rows, and some expert reaches 16. `held_expert`: A permutation of the experts. `swap_pairs`: 4 different values; value p stands for the slots p and p + 16.
All inputs are finite; a program needn't handle non-finite values.
Results may differ from a plain program's by a relative error of at most 0.02.
Values may be sent and summed in bfloat16 or wider, within the bound.
A program may use at most 128 MiB of HBM per device.

v0:
```python
import jax
import jax.numpy as jnp
from jax import lax
from jax.sharding import Mesh
from jax.sharding import PartitionSpec as P

DP = ("dp_0", "dp_1")
DP_EXPERT = ("dp_0", "dp_1", "expert")


beta_one = 0.9
beta_two = 0.95
learn_rate = 0.01
adam_eps = 1e-08
bias_one = 1.0 - 0.9**10
bias_two = 1.0 - 0.95**10


def passed_along(x, axis, by):
    length = lax.axis_size(axis)
    return lax.ppermute(x, axis, [(i, (i + by) % length) for i in range(length)])


def side_by_side(arrays, axis, dim, along):
    ends, at = ([], 0)
    for a in arrays[:-1]:
        at += a.shape[along]
        ends.append(at)
    both = jnp.concatenate(arrays, axis=along)
    return tuple(jnp.split(lax.all_gather(both, axis, axis=dim, tiled=True), ends, axis=along))


def side_by_side_2(arrays, axis, split_dim, concat_dim, along):
    widths = [a.shape[along] for a in arrays]
    both = jnp.concatenate(arrays, axis=along)
    result = lax.all_to_all(both, axis, split_axis=split_dim, concat_axis=concat_dim, tiled=True)
    return tuple(jnp.split(result, [sum(widths[:k]) for k in range(1, len(widths))], axis=along))


def own_block(parts, axes, turns):
    lengths = [lax.axis_size(a) for a in axes]
    parts = parts.reshape(*lengths, *parts.shape[1:])
    parts = parts.transpose(*turns, *range(len(axes), parts.ndim))
    parts = parts.reshape(-1, *parts.shape[len(axes) :])
    for k in turns:
        parts = lax.psum_scatter(parts, axes[k], scatter_dimension=0, tiled=True)
    return parts[0]


def split_up(x, dim, length):
    before, after = (x.shape[:dim], x.shape[dim + 1 :])
    return jnp.moveaxis(x.reshape(*before, length, -1, *after), dim, 0)


def scatter_axes(x, axes, turns, dim):
    length = lax.axis_size(axes)
    return own_block(split_up(x, dim, length), axes, turns)


def expert_pass(rows_x, rows_s, weight_in, weight_down):
    half_width = weight_down.shape[1]
    projected = jnp.dot(rows_x, weight_in, preferred_element_type=jnp.float32)
    gate_part = projected[:, :half_width]
    up_part = projected[:, half_width:]
    sigmoid = jax.nn.sigmoid(gate_part)
    activated = gate_part * sigmoid
    slope_term = sigmoid * (1.0 + gate_part * (1.0 - sigmoid))
    hidden = (activated * up_part).astype(jnp.bfloat16)
    expert_out = lax.dot_general(
        hidden, weight_down, (((1,), (1,)), ((), ())), preferred_element_type=jnp.float32
    ).astype(jnp.bfloat16)
    hidden_grad = jnp.dot(rows_s, weight_down, preferred_element_type=jnp.float32)
    pre_grad = jnp.concatenate(
        [hidden_grad * up_part * slope_term, hidden_grad * activated], axis=1
    ).astype(jnp.bfloat16)
    row_grad = lax.dot_general(
        pre_grad, weight_in, (((1,), (1,)), ((), ())), preferred_element_type=jnp.float32
    ).astype(jnp.bfloat16)
    grad_in = lax.dot_general(
        rows_x, pre_grad, (((0,), (0,)), ((), ())), preferred_element_type=jnp.float32
    )
    grad_down = lax.dot_general(
        rows_s, hidden, (((0,), (0,)), ((), ())), preferred_element_type=jnp.float32
    )
    return (row_grad, expert_out, grad_in, grad_down)


def adam_update(weight, first, second, grad):
    first_new = beta_one * first.astype(jnp.float32) + (1.0 - beta_one) * grad
    second_new = beta_two * second.astype(jnp.float32) + (1.0 - beta_two) * grad * grad
    step_size = first_new / bias_one / (jnp.sqrt(second_new / bias_two) + adam_eps)
    weight_new = weight.astype(jnp.float32) - learn_rate * step_size
    return (
        weight_new.astype(jnp.bfloat16),
        first_new.astype(jnp.bfloat16),
        second_new.astype(jnp.bfloat16),
    )


def body(
    tokens,
    out_grad,
    expert_ids,
    gate_probs,
    held_expert,
    swap_pairs,
    w_in,
    w_down,
    m_in,
    m_down,
    v_in,
    v_down,
):
    experts = lax.axis_size("expert")
    half_axis = experts // 2
    tok_rows = tokens.shape[0]
    top_count = expert_ids.shape[1]
    capacity = max(2, 2 * tok_rows * top_count // experts)
    room = experts * capacity
    slot_ids = jnp.arange(experts, dtype=jnp.int32)
    swap_flag = jnp.any((slot_ids % half_axis)[:, None] == swap_pairs[None, :], axis=1)
    mine_flag = swap_flag[lax.axis_index("expert")]
    held_after = jnp.where(swap_flag, jnp.roll(held_expert, half_axis), held_expert)
    states = (w_in, w_down, m_in, m_down, v_in, v_down)
    partner_states = passed_along(
        (states[0], states[1], states[2], states[3], states[4], states[5]), "expert", half_axis
    )
    states = tuple(
        (jnp.where(mine_flag, moved, kept) for moved, kept in zip(partner_states, states))
    )
    full_in, full_down = side_by_side((states[0], states[1]), DP, 1, 2)
    weight_in = full_in[0]
    weight_down = full_down[0]
    flat_ids = expert_ids.reshape(-1)
    pick_count = flat_ids.shape[0]
    target_slot = jnp.sum(
        jnp.where(held_after[None, :] == flat_ids[:, None], slot_ids[None, :], 0), axis=1
    )
    one_hot = (target_slot[:, None] == slot_ids[None, :]).astype(jnp.int32)
    earlier = jnp.cumsum(one_hot, axis=0) - one_hot
    position = jnp.sum(earlier * one_hot, axis=1)
    buffer_pos = target_slot * capacity + position
    pick_ids = jnp.arange(pick_count, dtype=jnp.int32)
    buffer_pick = jnp.full((room,), pick_count, jnp.int32).at[buffer_pos].set(pick_ids)
    buffer_token = buffer_pick // top_count
    scaled = (gate_probs[:, :, None] * out_grad[:, None, :].astype(jnp.float32)).astype(
        jnp.bfloat16
    )
    scaled = scaled.reshape(pick_count, -1)
    send_x = jnp.take(tokens, buffer_token, axis=0, mode="fill", fill_value=0).reshape(
        experts, capacity, -1
    )
    send_s = jnp.take(scaled, buffer_pick, axis=0, mode="fill", fill_value=0).reshape(
        experts, capacity, -1
    )
    recv_x, recv_s = side_by_side_2((send_x, send_s), "expert", 0, 0, 1)
    row_grad, expert_out, grad_in, grad_down = expert_pass(
        recv_x.reshape(room, -1), recv_s.reshape(room, -1), weight_in, weight_down
    )
    back_grad, back_out = side_by_side_2(
        (row_grad.reshape(experts, capacity, -1), expert_out.reshape(experts, capacity, -1)),
        "expert",
        0,
        0,
        1,
    )
    picked_grad = jnp.take(back_grad.reshape(room, -1), buffer_pos, axis=0)
    picked_out = jnp.take(back_out.reshape(room, -1), buffer_pos, axis=0)
    token_grad = jnp.sum(
        picked_grad.reshape(tok_rows, top_count, -1).astype(jnp.float32), axis=1
    ).astype(jnp.bfloat16)
    prob_grad = jnp.sum(
        picked_out.reshape(tok_rows, top_count, -1).astype(jnp.float32)
        * out_grad[:, None, :].astype(jnp.float32),
        axis=2,
    )
    sum_in, sum_down = (
        scatter_axes(grad_in.astype(jnp.bfloat16), DP, (1, 0), 0).astype(jnp.float32),
        scatter_axes(grad_down.astype(jnp.bfloat16), DP, (1, 0), 0).astype(jnp.float32),
    )
    new_w_in, new_m_in, new_v_in = adam_update(states[0], states[2], states[4], sum_in[None])
    new_w_down, new_m_down, new_v_down = adam_update(
        states[1], states[3], states[5], sum_down[None]
    )
    updated = (new_w_in, new_w_down, new_m_in, new_m_down, new_v_in, new_v_down)
    return (token_grad, prob_grad) + tuple(updated)


def solution(mesh):
    split = Mesh(mesh.devices.reshape(2, 4, mesh.shape["expert"]), ("dp_0", "dp_1", "expert"))
    placed = (
        P(DP_EXPERT, None),
        P(DP_EXPERT, None),
        P(DP_EXPERT, None),
        P(DP_EXPERT, None),
        P(),
        P(),
        P("expert", DP, None),
        P("expert", DP, None),
        P("expert", DP, None),
        P("expert", DP, None),
        P("expert", DP, None),
        P("expert", DP, None),
    )
    return jax.shard_map(
        body,
        mesh=split,
        in_specs=placed,
        out_specs=(
            P(DP_EXPERT, None),
            P(DP_EXPERT, None),
            P("expert", DP, None),
            P("expert", DP, None),
            P("expert", DP, None),
            P("expert", DP, None),
            P("expert", DP, None),
            P("expert", DP, None),
        ),
        check_vma=False,
    )
```

profile of v0, /device:TPU:33, one launch (start us, length us, event | category | flops | bytes accessed | tf_op | source)
XLA Modules:
  0.0 434.2 jit_solution(1369878463647337725)
XLA Ops:
  7.2 2.8 collective-permute-start
  10.3 0.7 compare_reduce_fusion
  11.0 0.7 dynamic_slice.3
  11.7 24.2 %collective-permute-done.1 = bf16[1,256,768]{2,1,0:T(8,128)(2,1)S(1)} collective-permute-done((bf16[1,256,768]{2,1,0:T(8,128)(2,1)}, bf16[1,256,768]{2,1,0:T(8,128)(2,1)S(1)}, u32[]{:S(2)}, u32[]{:S(2)}) %collective-permute-start.1) | collective-permute-done | bytes 393248 | tf_op jit(solution)/shard_map/ppermute | solution.py:21
  35.9 1.7 broadcast_select_fusion.8
  37.6 1.9 broadcast_select_fusion.5
  39.5 1.1 pad_maximum_fusion.3
  40.6 2.1 mul.146
  42.7 2.5 mul.147
  46.0 0.6 reduce-window.6
  46.9 1.4 scatter_custom_fusion
  48.6 1.8 multiply_convert_fusion
  50.3 3.3 gather_fusion.1
  53.7 3.4 gather_fusion
  57.0 1.9 broadcast_select_fusion
  59.0 0.6 pad_maximum_fusion
  59.6 153.3 %all_to_all.10 = bf16[32,32,2048]{2,1,0:T(8,128)(2,1)S(1)} all-to-all(bf16[32,32,2048]{2,1,0:T(8,128)(2,1)S(1)} %pad_maximum_fusion), channel_id=1, replica_groups=mesh['dp_0'=2,'dp_1'=4,'expert'=32] {'expert'}, dimensions={0} | all-to-all | bytes 8388608 | tf_op jit(solution)/shard_map/all_to_all | solution.py:36
  212.9 1.7 fusion.24
  214.6 22.2 %all-gather.2.cloned.1.call-done = bf16[1,2048,2304]{2,1,0:T(8,128)(2,1)} async-done(((bf16[1,256,2304]{2,1,0:T(8,128)(2,1)}), bf16[1,2048,2304]{2,1,0:T(8,128)(2,1)}) %all-gather.2.cloned.1.call-update) | async-done | bytes 9437200 | tf_op jit(solution)/shard_map/all_gather | solution.py:30
  236.9 5.6 %fusion.1 = f32[512,1536]{1,0:T(8,128)S(1)} fusion(bf16[512,2048]{1,0:T(8,128)(2,1)S(1)} %bitcast.65, bf16[1,2048,2304]{2,1,0:T(8,128)(2,1)} %all-gather.2.cloned.1.call-done), kind=kOutput, calls=%fused_computation.8 | convolution fusion | flops 3221225472 | bytes 11534336 | tf_op jit(solution)/shard_map/dot_general | solution.py:62
  242.5 5.2 %multiply_convert_fusion.3 = (bf16[512,768]{1,0:T(8,128)(2,1)}, bf16[512,768]{1,0:T(8,128)(2,1)}, bf16[512,768]{1,0:T(8,128)(2,1)S(1)}) fusion(f32[512,1536]{1,0:T(8,128)S(1)} %fusion.1, bf16[512,2048]{1,0:T(8,128)(2,1)S(1)} %bitcast.67, bf16[1,2048,2304]{2,1,0:T(8,128)(2,1)} %all-gather.2.cloned.1.call-done), kind=kOutput, calls=%fused_computation.28 | convolution fusion | flops 1616510976 | bytes 10747904 | tf_op jit(solution)/shard_map/dot_general | solution.py:72
  247.7 1.8 convolution_convert_fusion.1
  249.6 1.9 copy.32
  251.5 5.1 %convolution_convert_fusion = bf16[2048,1536]{1,0:T(8,128)(2,1)S(1)} fusion(bf16[512,2048]{1,0:T(8,128)(2,1)S(1)} %bitcast.66, bf16[512,768]{1,0:T(8,128)(2,1)} %get-tuple-element.30, bf16[512,768]{1,0:T(8,128)(2,1)} %get-tuple-element.29), kind=kOutput, calls=%fused_computation.5 | convolution fusion | flops 3227516928 | bytes 9961472 | tf_op jit(solution)/shard_map/dot_general | solution.py:79
  256.6 3.4 copy.31
  260.0 1.1 copy-done.13
  261.1 4.4 %convolution_convert_fusion.2 = bf16[512,2048]{1,0:T(8,128)(2,1)S(1)} fusion(bf16[512,768]{1,0:T(8,128)(2,1)S(1)} %copy-done.13, bf16[1,2048,2304]{2,1,0:T(8,128)(2,1)} %all-gather.2.cloned.1.call-done), kind=kOutput, calls=%fused_computation.14 | convolution fusion | flops 1611661312 | bytes 6029312 | tf_op jit(solution)/shard_map/dot_general | solution.py:69
  265.5 6.5 %fusion.2 = bf16[512,2048]{1,0:T(8,128)(2,1)S(1)} fusion(bf16[1,2048,2304]{2,1,0:T(8,128)(2,1)} %all-gather.2.cloned.1.call-done, bf16[512,768]{1,0:T(8,128)(2,1)S(1)} %copy-done.15, bf16[512,768]{1,0:T(8,128)(2,1)S(1)} %copy-done.14), kind=kOutput, calls=%fused_computation.13 | convolution fusion | flops 3225419776 | bytes 9961472 | tf_op jit(solution)/shard_map/dot_general | solution.py:76
  272.0 2.6 pad_maximum_fusion.1
  274.6 10.1 %all-to-all-start.1 = ((bf16[32,32,2048]{2,1,0:T(8,128)(2,1)}), bf16[32,32,2048]{2,1,0:T(8,128)(2,1)}, u32[]{:S(2)}, u32[]{:S(2)}) async-start(bf16[32,32,2048]{2,1,0:T(8,128)(2,1)} %pad_maximum_fusion.1), calls=%async_computation.1 | async-start | bytes 8388608 | tf_op jit(solution)/shard_map/all_to_all | solution.py:36
  284.7 6.9 %reduce-scatter.9.cloned.1.call-done = bf16[2,256,768]{2,1,0:T(8,128)(2,1)} async-done(((bf16[8,256,768]{2,1,0:T(8,128)(2,1)}), bf16[2,256,768]{2,1,0:T(8,128)(2,1)}) %reduce-scatter.9.cloned.1.call-update) | async-done | bytes 786448 | tf_op jit(solution)/shard_map/reduce_scatter | solution.py:46
  291.7 68.8 %reduce-scatter.5.cloned.1.call-done = bf16[2,256,1536]{2,1,0:T(8,128)(2,1)} async-done(((bf16[8,256,1536]{2,1,0:T(8,128)(2,1)}), bf16[2,256,1536]{2,1,0:T(8,128)(2,1)}) %reduce-scatter.5.cloned.1.call-update) | async-done | bytes 1572880 | tf_op jit(solution)/shard_map/reduce_scatter | solution.py:46
  360.6 2.8 collective-permute-start.5
  363.7 2.6 collective-permute-start.3
  366.7 11.5 %collective-permute-done.5 = bf16[1,256,768]{2,1,0:T(8,128)(2,1)S(1)} collective-permute-done((bf16[1,256,768]{2,1,0:T(8,128)(2,1)S(1)}, bf16[1,256,768]{2,1,0:T(8,128)(2,1)S(1)}, u32[]{:S(2)}, u32[]{:S(2)}) %collective-permute-start.5) | collective-permute-done | bytes 393248 | tf_op jit(solution)/shard_map/ppermute | solution.py:21
  378.2 10.2 %collective-permute-done.4 = bf16[1,256,768]{2,1,0:T(8,128)(2,1)S(1)} collective-permute-done((bf16[1,256,768]{2,1,0:T(8,128)(2,1)S(1)}, bf16[1,256,768]{2,1,0:T(8,128)(2,1)S(1)}, u32[]{:S(2)}, u32[]{:S(2)}) %collective-permute-start.4) | collective-permute-done | bytes 393248 | tf_op jit(solution)/shard_map/ppermute | solution.py:21
  388.4 0.9 reduce-scatter.11.cloned.1.call-done
  389.2 3.6 fusion.12
  392.8 4.0 fusion.23
  396.8 5.2 %gather_fusion.2 = bf16[256,2048]{1,0:T(8,128)(2,1)} fusion(bf16[512,2048]{1,0:T(8,128)(2,1)} %bitcast.58, s32[1024]{0:T(1024)S(1)} %pad_clamp_fusion), kind=kCustom, calls=%fused_computation.clone | custom fusion | bytes 2098176 | tf_op jit(solution)/shard_map/jit(_take)/gather | solution.py:167
  402.1 2.4 broadcast_select_fusion.2
  404.5 2.5 reshape.148
  407.0 2.4 gather_fusion.3
  409.4 2.4 multiply_reduce_fusion
  411.9 0.6 copy.33
  412.5 3.6 reduce_sum.43
  416.2 6.0 %collective-permute-done.2 = bf16[1,256,1536]{2,1,0:T(8,128)(2,1)} collective-permute-done((bf16[1,256,1536]{2,1,0:T(8,128)(2,1)}, bf16[1,256,1536]{2,1,0:T(8,128)(2,1)}, u32[]{:S(2)}, u32[]{:S(2)}) %collective-permute-start.2) | collective-permute-done | bytes 786464 | tf_op jit(solution)/shard_map/ppermute | solution.py:21
  422.2 5.5 %fusion.8 = (bf16[1,256,1536]{2,1,0:T(8,128)(2,1)}, bf16[1,256,1536]{2,1,0:T(8,128)(2,1)}, bf16[1,256,1536]{2,1,0:T(8,128)(2,1)}) fusion(bf16[1,256,1536]{2,1,0:T(8,128)(2,1)} %reduce-scatter.7.cloned.1.call-done, bf16[1,256,1536]{2,1,0:T(8,128)(2,1)} %collective-permute-done.3, bf16[1,256,1536]{2,1,0:T(8,128)(2,1)} %param.24, pred[]{:T(512)} %bitcast.7, ...), kind=kLoop, calls=%fused_computation.32 | loop fusion | flops 8650752 | bytes 7077889 | tf_op jit(solution)/shard_map/convert_element_type | solution.py:96
  (73 shorter events, 2.7 us)
Async XLA Ops:
  7.2 46.5 %copy-start = (bf16[128,2048]{1,0:T(8,128)(2,1)S(1)}, bf16[128,2048]{1,0:T(8,128)(2,1)}, u32[]{:S(2)}) copy-start(bf16[128,2048]{1,0:T(8,128)(2,1)} %param.14) | copy-start | bytes 1572868
  7.2 229.7 %all-gather.2.cloned.1.call-start = ((), (), s32[]{:S(2)}) async-start(), calls=%async_computation.6 | async-start | bytes 10616832 | tf_op jit(solution)/shard_map/all_gather | solution.py:30
  7.2 30.3 %collective-permute-start = (bf16[1,256,1536]{2,1,0:T(8,128)(2,1)}, bf16[1,256,1536]{2,1,0:T(8,128)(2,1)S(1)}, u32[]{:S(2)}, u32[]{:S(2)}) collective-permute-start(bf16[1,256,1536]{2,1,0:T(8,128)(2,1)} %param.20), channel_id=1, source_target_pairs={{0,16},{1,17},{2,18},{3,19},{4,20},{5,21},{6,22},{7,23},{8,24},{9,... | collective-permute-start | bytes 2359304 | tf_op jit(solution)/shard_map/ppermute | solution.py:21
  10.1 25.8 %collective-permute-start.1 = (bf16[1,256,768]{2,1,0:T(8,128)(2,1)}, bf16[1,256,768]{2,1,0:T(8,128)(2,1)S(1)}, u32[]{:S(2)}, u32[]{:S(2)}) collective-permute-start(bf16[1,256,768]{2,1,0:T(8,128)(2,1)} %param.21), channel_id=1, source_target_pairs={{0,16},{1,17},{2,18},{3,19},{4,20},{5,21},{6,22},{7,23},{8,24},{9,... | collective-permute-start | bytes 1179656 | tf_op jit(solution)/shard_map/ppermute | solution.py:21
  37.6 1.9 copy-start.4
  40.6 251.0 %reduce-scatter.9.cloned.1.call-start = ((), (), s32[]{:S(2)}) async-start(), calls=%async_computation.9 | async-start | bytes 3932160 | tf_op jit(solution)/shard_map/reduce_scatter | solution.py:46
  42.7 2.5 copy-start.10
  42.7 2.7 copy-start.11
  42.7 3.0 copy-start.9
  53.7 3.4 copy-start.2
  236.9 5.7 %copy-start.6 = (bf16[32,16,2048]{2,1,0:T(8,128)(2,1)S(1)}, bf16[32,16,2048]{2,1,0:T(8,128)(2,1)}, u32[]{:S(2)}) copy-start(bf16[32,16,2048]{2,1,0:T(8,128)(2,1)} %get-tuple-element.33) | copy-start | bytes 6291460
  247.7 1.8 copy-start.12
  251.5 109.0 %reduce-scatter.5.cloned.1.call-start = ((), (), s32[]{:S(2)}) async-start(), calls=%async_computation.7 | async-start | bytes 7864320 | tf_op jit(solution)/shard_map/reduce_scatter | solution.py:46
  260.0 1.1 copy-start.13
  261.1 4.4 %copy-start.14 = (bf16[512,768]{1,0:T(8,128)(2,1)S(1)}, bf16[512,768]{1,0:T(8,128)(2,1)}, u32[]{:S(2)}) copy-start(bf16[512,768]{1,0:T(8,128)(2,1)} %get-tuple-element.29) | copy-start | bytes 2359300
  261.1 4.4 %copy-start.15 = (bf16[512,768]{1,0:T(8,128)(2,1)S(1)}, bf16[512,768]{1,0:T(8,128)(2,1)}, u32[]{:S(2)}) copy-start(bf16[512,768]{1,0:T(8,128)(2,1)} %get-tuple-element.30) | copy-start | bytes 2359300
  274.6 118.2 %all-to-all-start.1 = ((bf16[32,32,2048]{2,1,0:T(8,128)(2,1)}), bf16[32,32,2048]{2,1,0:T(8,128)(2,1)}, u32[]{:S(2)}, u32[]{:S(2)}) async-start(bf16[32,32,2048]{2,1,0:T(8,128)(2,1)} %pad_maximum_fusion.1), calls=%async_computation.1 | async-start | bytes 8388608 | tf_op jit(solution)/shard_map/all_to_all | solution.py:36
  284.7 75.9 %copy-start.7 = (bf16[1,256,768]{2,1,0:T(8,128)(2,1)S(1)}, bf16[1,256,768]{2,1,0:T(8,128)(2,1)}, u32[]{:S(2)}) copy-start(bf16[1,256,768]{2,1,0:T(8,128)(2,1)} %param.25) | copy-start | bytes 1179652
  284.7 78.7 %copy-start.8 = (bf16[1,256,768]{2,1,0:T(8,128)(2,1)S(1)}, bf16[1,256,768]{2,1,0:T(8,128)(2,1)}, u32[]{:S(2)}) copy-start(bf16[1,256,768]{2,1,0:T(8,128)(2,1)} %param.23) | copy-start | bytes 1179652
  284.7 104.6 %copy-start.5 = (bf16[1,256,768]{2,1,0:T(8,128)(2,1)S(1)}, bf16[1,256,768]{2,1,0:T(8,128)(2,1)}, u32[]{:S(2)}) copy-start(bf16[1,256,768]{2,1,0:T(8,128)(2,1)} %copy-done.4) | copy-start | bytes 1179652
  284.7 104.5 %reduce-scatter.11.cloned.1.call-start = ((), (), s32[]{:S(2)}) async-start(), calls=%async_computation.10 | async-start | bytes 1179648 | tf_op jit(solution)/shard_map/reduce_scatter | solution.py:46
  291.6 130.6 %reduce-scatter.7.cloned.1.call-start = ((), (), s32[]{:S(2)}) async-start(), calls=%async_computation.8 | async-start | bytes 2359296 | tf_op jit(solution)/shard_map/reduce_scatter | solution.py:46
  360.6 17.6 %collective-permute-start.5 = (bf16[1,256,768]{2,1,0:T(8,128)(2,1)S(1)}, bf16[1,256,768]{2,1,0:T(8,128)(2,1)S(1)}, u32[]{:S(2)}, u32[]{:S(2)}) collective-permute-start(bf16[1,256,768]{2,1,0:T(8,128)(2,1)S(1)} %copy-done.7), channel_id=1, source_target_pairs={{0,16},{1,17},{2,18},{3,19},{4,20},{5,21},{6,22},{7,23},{8,24},{9,... | collective-permute-start | bytes 1179656 | tf_op jit(solution)/shard_map/ppermute | solution.py:21
  363.4 25.0 %collective-permute-start.4 = (bf16[1,256,768]{2,1,0:T(8,128)(2,1)S(1)}, bf16[1,256,768]{2,1,0:T(8,128)(2,1)S(1)}, u32[]{:S(2)}, u32[]{:S(2)}) collective-permute-start(bf16[1,256,768]{2,1,0:T(8,128)(2,1)S(1)} %copy-done.8), channel_id=1, source_target_pairs={{0,16},{1,17},{2,18},{3,19},{4,20},{5,21},{6,22},{7,23},{8,24},{9,... | collective-permute-start | bytes 1179656 | tf_op jit(solution)/shard_map/ppermute | solution.py:21
  363.7 52.5 %collective-permute-start.3 = (bf16[1,256,1536]{2,1,0:T(8,128)(2,1)}, bf16[1,256,1536]{2,1,0:T(8,128)(2,1)}, u32[]{:S(2)}, u32[]{:S(2)}) collective-permute-start(bf16[1,256,1536]{2,1,0:T(8,128)(2,1)} %param.24), channel_id=1, source_target_pairs={{0,16},{1,17},{2,18},{3,19},{4,20},{5,21},{6,22},{7,23},{8,24},{9,... | collective-permute-start | bytes 2359304 | tf_op jit(solution)/shard_map/ppermute | solution.py:21
  366.3 55.9 %collective-permute-start.2 = (bf16[1,256,1536]{2,1,0:T(8,128)(2,1)}, bf16[1,256,1536]{2,1,0:T(8,128)(2,1)}, u32[]{:S(2)}, u32[]{:S(2)}) collective-permute-start(bf16[1,256,1536]{2,1,0:T(8,128)(2,1)} %param.22), channel_id=1, source_target_pairs={{0,16},{1,17},{2,18},{3,19},{4,20},{5,21},{6,22},{7,23},{8,24},{9,... | collective-permute-start | bytes 2359304 | tf_op jit(solution)/shard_map/ppermute | solution.py:21
  409.4 3.2 copy-start.3
  412.5 15.2 %copy-start.1 = (bf16[128,2048]{1,0:T(8,128)(2,1)S(1)}, bf16[128,2048]{1,0:T(8,128)(2,1)}, u32[]{:S(2)}) copy-start(bf16[128,2048]{1,0:T(8,128)(2,1)} %param.14) | copy-start | bytes 1572868
Sparse Core Ops, SparseCore 0:
  40.7 196.1 all-gather.1
  251.6 39.9 reduce-scatter.8
  294.2 66.2 reduce-scatter.4
  362.9 26.3 reduce-scatter.10
  391.6 25.8 reduce-scatter.6
where the time goes:
time: 439 us; the launch traced here: 434 us
  blocking collectives  153 us (35%)
  waiting for transfers between devices  151 us (34%)
  local copies, waits for them, and re-layouts  37.3 us (8%)
  other arithmetic  30.6 us (7%)
  matrix products  28.6 us (7%)
  starting transfers between devices  19.4 us (4%)
  between operations  14.1 us (3%)
    all_to_all x1, blocking collectives, side_by_side_2(): lax.all_to_all(both, axis, split_axis=split_dim, concat_axis=concat_dim,...  153 us
    reduce_scatter x4, waiting for transfers between devices, own_block(): parts = lax.psum_scatter(parts, axes[k], scatter_dimension=0, tiled=True)  76.6 us
    ppermute x6, waiting for transfers between devices, passed_along(): lax.ppermute(x, axis, [(i, (i + by) % length) for i in range(length)])  51.9 us
    all_gather x1, waiting for transfers between devices, side_by_side(): lax.all_gather(both, axis, axis=dim, tiled=True)  22.2 us
    all_to_all x1, starting transfers between devices, side_by_side_2(): lax.all_to_all(both, axis, split_axis=split_dim, concat_axis=concat_dim,...  10.1 us
    ppermute x6, starting transfers between devices, passed_along(): lax.ppermute(x, axis, [(i, (i + by) % length) for i in range(length)])  9.15 us
    convert_element_type x2, other arithmetic, adam_update(): second_new.astype(jnp.bfloat16)  9.06 us
  transfers between devices with their start and end apart: 12, of which 8 were waited for; matrix products, arithmetic and copies ran while one was open for 17% of the time, Pallas kernels for 0%

commit v1 on v0

v1 whole, which is shorter than its diff:
```python
import functools

import jax
import jax.numpy as jnp
from jax import lax
from jax.experimental import pallas as pl
from jax.experimental.pallas import tpu as pltpu
from jax.sharding import Mesh
from jax.sharding import PartitionSpec as P

DP = ("dp_0", "dp_1")
DP_EXPERT = ("dp_0", "dp_1", "expert")
MESH = pl.DeviceIdType.MESH
BF16, F32 = jnp.bfloat16, jnp.float32

beta_one = 0.9
beta_two = 0.95
learn_rate = 0.01
adam_eps = 1e-08
bias_one = 1.0 - 0.9**10
bias_two = 1.0 - 0.95**10

LANES = 128
GATHER_CHUNKS = 2
SUM_CHUNKS = 4
EARLY_SENDS = 10
VMEM_BYTES = 60 * 1024 * 1024


def in_parts(column):
    high = column.astype(BF16).astype(F32)
    rest = column - high
    middle = rest.astype(BF16).astype(F32)
    low = rest - middle
    lane = lax.broadcasted_iota(jnp.int32, (column.shape[0], LANES), 1)
    low = jnp.where(lane == 2, low, 0.0)
    return jnp.where(lane == 0, high, jnp.where(lane == 1, middle, low)).astype(BF16)


def from_parts(parts):
    parts = parts.astype(F32)
    return parts[:, 0:1] + parts[:, 1:2] + parts[:, 2:3]


def dot(a, b, contract=(1, 0)):
    dims = (((contract[0],), (contract[1],)), ((), ()))
    return lax.dot_general(a, b, dims, preferred_element_type=F32)


def swapped_here(pairs_ref, me, half_axis):
    mine = lax.rem(me, half_axis)
    flag = (mine == pairs_ref[0]).astype(jnp.int32)
    for j in range(1, pairs_ref.shape[0]):
        flag = jnp.maximum(flag, (mine == pairs_ref[j]).astype(jnp.int32))
    return flag


def choose(flag, moved, kept):
    return jnp.where(jnp.full(kept.shape, flag, jnp.int32) > 0, moved.astype(F32), kept.astype(F32))


def send(source, target, sems, at, device):
    return pltpu.make_async_remote_copy(
        src_ref=source,
        dst_ref=target,
        send_sem=sems[0].at[at],
        recv_sem=sems[1].at[at],
        device_id=device,
        device_id_type=MESH,
    )


class Place:
    def __init__(self):
        self.z, self.y = lax.axis_index("dp_0"), lax.axis_index("dp_1")
        self.me = lax.axis_index("expert")
        self.layers, self.ring = lax.axis_size("dp_0"), lax.axis_size("dp_1")
        self.experts = lax.axis_size("expert")
        self.across = {"dp_0": 1 - self.z}
        self.up = {"dp_1": lax.rem(self.y + 1, self.ring)}
        self.down = {"dp_1": lax.rem(self.y + self.ring - 1, self.ring)}

    def later(self, k):
        return {"expert": lax.rem(self.me + k, self.experts)}

    def offset(self, i):
        return (i % 2) * ((i + 1) // 2) + (1 - i % 2) * (self.experts - i // 2)

    def shard(self, layer, step):
        z = (self.z + layer) % self.layers
        return z * self.ring + (self.y + step) % self.ring

    def greet(self):
        barrier = pltpu.get_barrier_semaphore()

        def hello(k, carry):
            pl.semaphore_signal(barrier, inc=1, device_id=self.later(k), device_id_type=MESH)
            return carry

        lax.fori_loop(1, self.experts, hello, 0)
        for device in (self.across, self.up, self.down):
            pl.semaphore_signal(barrier, inc=1, device_id=device, device_id_type=MESH)
        pl.semaphore_wait(barrier, self.experts - 1 + 3)


def gather_kernel(
    ids_ref, held_ref, pairs_ref, probs_ref, tokens_ref, grads_ref, w_in_ref, w_down_ref,
    recv_ref, full_ref, hots_ref,
    send_ref, swap_in, swap_down, row_send, row_recv, swap_send, swap_recv, ring_send, ring_recv,
):
    at = Place()
    experts, half_axis = at.experts, at.experts // 2
    tok_rows, width = tokens_ref.shape
    room = send_ref.shape[0]
    capacity = room // experts
    wide = w_in_ref.shape[1]
    depth = w_in_ref.shape[0]
    part = depth // GATHER_CHUNKS
    at.greet()

    partner = at.later(half_axis)
    sems = (swap_send, swap_recv)
    swaps = []
    for c in range(GATHER_CHUNKS):
        rows = pl.ds(c * part, part)
        swaps.append(
            (
                send(w_in_ref.at[rows], swap_in.at[rows], sems, (0, c), partner),
                send(w_down_ref.at[rows], swap_down.at[rows], sems, (1, c), partner),
            )
        )
        for copy in swaps[-1]:
            copy.start()

    slot = lax.broadcasted_iota(jnp.int32, (experts, 1), 0)
    flag = (slot % half_axis == pairs_ref[0]).astype(jnp.int32)
    for j in range(1, pairs_ref.shape[0]):
        flag = jnp.maximum(flag, (slot % half_axis == pairs_ref[j]).astype(jnp.int32))
    held = jnp.where(flag > 0, held_ref[:, 1:2], held_ref[:, 0:1])
    hits = [(ids_ref[k : k + 1, :] == held).astype(F32) for k in range(ids_ref.shape[0])]
    named = hits[0]
    for hit in hits[1:]:
        named = named + hit
    row = lax.broadcasted_iota(jnp.int32, (tok_rows, tok_rows), 0)
    column = lax.broadcasted_iota(jnp.int32, (tok_rows, tok_rows), 1)
    before = dot(named.astype(BF16), (row < column).astype(F32).astype(BF16))
    first = (((slot + experts - at.me) % experts) * capacity).astype(F32)
    room_ids = lax.broadcasted_iota(jnp.int32, (room, tok_rows), 0)
    parts = jnp.zeros((room, LANES), F32)
    both = jnp.zeros((room, tok_rows), F32)
    for k, hit in enumerate(hits):
        place = jnp.sum(hit * (before + first), axis=0, keepdims=True).astype(jnp.int32)
        hot = (room_ids == place).astype(F32)
        hots_ref[k] = hot.astype(BF16)
        both = both + hot
        parts = parts + dot(hot.astype(BF16), in_parts(probs_ref[:, k : k + 1]))
    send_ref[:, 2 * width :] = parts.astype(BF16)
    both = both.astype(BF16)
    step = min(512, width)
    for c in range(width // step):
        columns = pl.ds(c * step, step)
        send_ref[:, columns] = dot(both, tokens_ref[:, columns]).astype(BF16)
        send_ref[:, pl.ds(width + c * step, step)] = dot(both, grads_ref[:, columns]).astype(BF16)

    def rows_to(i):
        k = at.offset(i)
        rows = pl.ds(k * capacity, capacity)
        copy = pltpu.make_async_remote_copy(
            src_ref=send_ref.at[rows],
            dst_ref=recv_ref.at[rows],
            send_sem=row_send.at[k],
            recv_sem=row_recv.at[k],
            device_id=at.later(k),
            device_id_type=MESH,
        )
        return copy

    def start_rows(i, carry):
        rows_to(i).start()
        return carry

    def wait_rows(i, carry):
        rows_to(i).wait()
        return carry

    early = min(EARLY_SENDS, experts - 1)
    lax.fori_loop(1, 1 + early, start_rows, 0)
    recv_ref[0:capacity] = send_ref[0:capacity]

    flag = swapped_here(pairs_ref, at.me, half_axis)
    ring = (ring_send, ring_recv)

    def shard(layer, step, c):
        start = at.shard(layer, step) * depth + c * part
        return full_ref.at[pl.ds(pl.multiple_of(start, part), part)]

    def spread(kind, layer, step, c, device):
        block = shard(layer, step, c)
        return send(block, block, ring, (kind, c), device)

    sent = []

    def begin(*what):
        copy = spread(*what)
        copy.start()
        sent.append(copy)

    ACROSS, UP_OWN, DOWN_OWN, UP_OTHER, DOWN_OTHER, UP_ON, DOWN_ON = range(7)
    for c in range(GATHER_CHUNKS):
        for copy in swaps[c]:
            copy.wait_recv()
        rows = pl.ds(c * part, part)
        mine = shard(0, 0, c)
        mine[:, pl.ds(0, wide)] = choose(flag, swap_in[rows], w_in_ref[rows]).astype(BF16)
        mine[:, pl.ds(wide, w_down_ref.shape[1])] = choose(
            flag, swap_down[rows], w_down_ref[rows]
        ).astype(BF16)
        begin(ACROSS, 0, 0, c, at.across)
        begin(UP_OWN, 0, 0, c, at.up)
        begin(DOWN_OWN, 0, 0, c, at.down)
    lax.fori_loop(1 + early, experts, start_rows, 0)
    for c in range(GATHER_CHUNKS):
        spread(UP_OWN, 0, -1, c, at.up).wait_recv()
        begin(UP_ON, 0, -1, c, at.up)
        spread(ACROSS, 1, 0, c, at.across).wait_recv()
        begin(UP_OTHER, 1, 0, c, at.up)
        begin(DOWN_OTHER, 1, 0, c, at.down)
    for c in range(GATHER_CHUNKS):
        spread(DOWN_OTHER, 1, 1, c, at.down).wait_recv()
        begin(DOWN_ON, 1, 1, c, at.down)
    lax.fori_loop(1, experts, wait_rows, 0)
    for c in range(GATHER_CHUNKS):
        spread(DOWN_OWN, 0, 1, c, at.down).wait_recv()
        spread(UP_OTHER, 1, -1, c, at.up).wait_recv()
        spread(UP_ON, 0, -2, c, at.up).wait_recv()
        spread(DOWN_ON, 1, 2, c, at.down).wait_recv()
        for copy in swaps[c]:
            copy.wait_send()
    for copy in sent:
        copy.wait_send()


def expert_kernel(
    recv_ref, full_ref, hots_ref, pairs_ref, m_in_ref, m_down_ref, v_in_ref, v_down_ref,
    token_ref, prob_ref, nw_in, nw_down, nm_in, nm_down, nv_in, nv_down,
    scaled, pre, hidden, grad, ret, back, on_up, on_down,
    a_low, a_high, b_low, b_high, z_out, z_in, pm_in, pm_down, pv_in, pv_down,
    row_send, row_recv, swap_send, swap_recv, ring_send, ring_recv,
):
    at = Place()
    experts, half_axis = at.experts, at.experts // 2
    room = recv_ref.shape[0]
    capacity = room // experts
    width = token_ref.shape[1]
    half_width = hidden.shape[1]
    wide = 2 * half_width
    depth = m_in_ref.shape[0]
    part = depth // SUM_CHUNKS
    at.greet()

    partner = at.later(half_axis)
    swaps = []
    for n, (own, other) in enumerate(
        ((m_in_ref, pm_in), (m_down_ref, pm_down), (v_in_ref, pv_in), (v_down_ref, pv_down))
    ):
        swaps.append(send(own, other, (swap_send, swap_recv), n, partner))
        swaps[-1].start()

    rows_p = from_parts(recv_ref[:, 2 * width :])
    step = min(512, width)
    for c in range(width // step):
        columns = pl.ds(c * step, step)
        rows_g = recv_ref[:, pl.ds(width + c * step, step)].astype(F32)
        scaled[:, columns] = (rows_p * rows_g).astype(BF16)
    block = min(256, half_width)

    def through(n, carry):
        gate_at = pl.multiple_of(n * block, block)
        up_at = pl.multiple_of(half_width + n * block, block)
        down_at = pl.multiple_of(wide + n * block, block)
        gate_part = dot(recv_ref[:, :width], full_ref[:, pl.ds(gate_at, block)])
        up_part = dot(recv_ref[:, :width], full_ref[:, pl.ds(up_at, block)])
        hidden_grad = dot(scaled[...], full_ref[:, pl.ds(down_at, block)])
        sigmoid = jax.nn.sigmoid(gate_part)
        activated = gate_part * sigmoid
        slope_term = sigmoid * (1.0 + gate_part * (1.0 - sigmoid))
        hidden[:, pl.ds(gate_at, block)] = (activated * up_part).astype(BF16)
        pre[:, pl.ds(gate_at, block)] = (hidden_grad * up_part * slope_term).astype(BF16)
        pre[:, pl.ds(up_at, block)] = (hidden_grad * activated).astype(BF16)
        return carry

    lax.fori_loop(0, half_width // block, through, 0)

    def weight_grads(i, carry):
        start = pl.multiple_of(at.shard(i % 2, 2 + i // 2) * depth, depth)
        columns = pl.ds(start, depth)
        grad[i, :, pl.ds(0, wide)] = dot(recv_ref[:, columns], pre[...], (0, 0)).astype(BF16)
        grad[i, :, pl.ds(wide, half_width)] = dot(
            scaled[:, columns], hidden[...], (0, 0)
        ).astype(BF16)
        return carry

    ring = (ring_send, ring_recv)
    sent = []

    def begin(source, target, kind, c, device):
        copy = send(source, target.at[c], ring, (kind, c), device)
        copy.start()
        sent.append(copy)

    def arrived(target, kind, c):
        send(target.at[c], target.at[c], ring, (kind, c), at.up).wait_recv()
        return target[c].astype(F32)

    def rows_of(c):
        return pl.ds(c * part, part)

    A2, B2, A3, B3, A0, B0, A1, B1 = range(8)
    ON_UP, ON_DOWN, A_LOW, A_HIGH, B_LOW, B_HIGH, Z = range(7)
    lax.fori_loop(0, 2, weight_grads, 0)
    for c in range(SUM_CHUNKS):
        begin(grad.at[A2, rows_of(c)], on_up, ON_UP, c, at.up)
        begin(grad.at[B2, rows_of(c)], on_down, ON_DOWN, c, at.down)
    lax.fori_loop(2, 8, weight_grads, 0)
    early = SUM_CHUNKS // 2
    for c in range(early):
        begin(grad.at[B1, rows_of(c)], b_low, B_LOW, c, at.up)
        begin(grad.at[A3, rows_of(c)], a_high, A_HIGH, c, at.down)

    block = min(256, width)

    def row_grads(n, total):
        start = pl.multiple_of(n * block, block)
        rows = pl.ds(start, block)
        ret[:, rows] = dot(pre[...], full_ref[rows, pl.ds(0, wide)], (1, 1)).astype(BF16)
        out = dot(hidden[...], full_ref[rows, pl.ds(wide, half_width)], (1, 1)).astype(BF16)
        rows_g = recv_ref[:, pl.ds(pl.multiple_of(width + start, block), block)].astype(F32)
        return total + jnp.sum(out.astype(F32) * rows_g, axis=1, keepdims=True)

    total = lax.fori_loop(0, width // block, row_grads, jnp.zeros((room, 1), F32))
    ret[:, width:] = in_parts(total)

    def rows_to(i):
        k = at.offset(i)
        rows = pl.ds(k * capacity, capacity)
        return pltpu.make_async_remote_copy(
            src_ref=ret.at[rows],
            dst_ref=back.at[rows],
            send_sem=row_send.at[k],
            recv_sem=row_recv.at[k],
            device_id=at.later(experts - k),
            device_id_type=MESH,
        )

    def start_rows(i, carry):
        rows_to(i).start()
        return carry

    def wait_rows(i, carry):
        rows_to(i).wait()
        return carry

    lax.fori_loop(1, experts, start_rows, 0)
    back[0:capacity] = ret[0:capacity]

    def pass_on(c):
        low = grad[A1, rows_of(c)].astype(F32) + arrived(on_up, ON_UP, c)
        grad[A1, rows_of(c)] = low.astype(BF16)
        begin(grad.at[A1, rows_of(c)], a_low, A_LOW, c, at.up)
        high = grad[B3, rows_of(c)].astype(F32) + arrived(on_down, ON_DOWN, c)
        grad[B3, rows_of(c)] = high.astype(BF16)
        begin(grad.at[B3, rows_of(c)], b_high, B_HIGH, c, at.down)

    for c in range(SUM_CHUNKS):
        pass_on(c)
        if c + early < SUM_CHUNKS:
            begin(grad.at[B1, rows_of(c + early)], b_low, B_LOW, c + early, at.up)
            begin(grad.at[A3, rows_of(c + early)], a_high, A_HIGH, c + early, at.down)

    def hand_over(c):
        mine = grad[B0, rows_of(c)].astype(F32)
        mine = mine + arrived(b_low, B_LOW, c) + arrived(b_high, B_HIGH, c)
        z_out[c] = mine.astype(BF16)
        begin(z_out.at[c], z_in, Z, c, at.across)

    flag = swapped_here(pairs_ref, at.me, half_axis)

    def adam(c):
        rows = rows_of(c)
        mine = grad[A0, rows].astype(F32)
        mine = mine + arrived(a_low, A_LOW, c) + arrived(a_high, A_HIGH, c)
        mine = mine + arrived(z_in, Z, c)
        own = pl.ds(pl.multiple_of(at.shard(0, 0) * depth + c * part, part), part)
        for columns, refs in (
            (pl.ds(0, wide), (pm_in, m_in_ref, pv_in, v_in_ref, nw_in, nm_in, nv_in)),
            (
                pl.ds(wide, half_width),
                (pm_down, m_down_ref, pv_down, v_down_ref, nw_down, nm_down, nv_down),
            ),
        ):
            value = mine[:, columns.start : columns.start + columns.size]
            first = choose(flag, refs[0][rows], refs[1][rows])
            second = choose(flag, refs[2][rows], refs[3][rows])
            weight = full_ref[own, columns].astype(F32)
            first_new = beta_one * first + (1.0 - beta_one) * value
            second_new = beta_two * second + (1.0 - beta_two) * value * value
            step_size = first_new / bias_one / (jnp.sqrt(second_new / bias_two) + adam_eps)
            refs[4][rows] = (weight - learn_rate * step_size).astype(BF16)
            refs[5][rows] = first_new.astype(BF16)
            refs[6][rows] = second_new.astype(BF16)

    for c in range(early):
        hand_over(c)
    for copy in swaps:
        copy.wait()
    lax.fori_loop(1, experts, wait_rows, 0)
    hots = [hots_ref[k] for k in range(hots_ref.shape[0])]
    both = hots[0]
    for hot in hots[1:]:
        both = both + hot
    step = min(512, width)
    for c in range(width // step):
        columns = pl.ds(c * step, step)
        token_ref[:, columns] = dot(both, back[:, columns], (0, 0)).astype(BF16)
    for k, hot in enumerate(hots):
        prob_ref[:, k : k + 1] = from_parts(dot(hot, back[:, width:], (0, 0)))
    for c in range(early, SUM_CHUNKS):
        hand_over(c)
        adam(c - early)
    for c in range(SUM_CHUNKS - early, SUM_CHUNKS):
        adam(c)
    for copy in sent:
        copy.wait_send()


def body(
    tokens,
    out_grad,
    expert_ids,
    gate_probs,
    held_expert,
    swap_pairs,
    w_in,
    w_down,
    m_in,
    m_down,
    v_in,
    v_down,
):
    experts = lax.axis_size("expert")
    dp = lax.axis_size(DP)
    tok_rows, width = tokens.shape
    top_count = expert_ids.shape[1]
    capacity = max(2, 2 * tok_rows * top_count // experts)
    room = experts * capacity
    _, depth, wide = w_in.shape
    half_width = w_down.shape[2]
    row_width = 2 * width + LANES
    held = jnp.stack([held_expert, jnp.roll(held_expert, experts // 2)], axis=1)
    vmem = pl.BlockSpec(memory_space=pltpu.VMEM)
    smem = pl.BlockSpec(memory_space=pltpu.SMEM)
    dma = pltpu.SemaphoreType.DMA
    shape = jax.ShapeDtypeStruct
    part = depth // GATHER_CHUNKS
    recv, full, hots = pl.pallas_call(
        gather_kernel,
        name="gather",
        out_shape=(
            shape((room, row_width), BF16),
            shape((dp * depth, wide + half_width), BF16),
            shape((top_count, room, tok_rows), BF16),
        ),
        in_specs=[vmem, vmem, smem, vmem, vmem, vmem, vmem, vmem],
        out_specs=(vmem,) * 3,
        scratch_shapes=[
            pltpu.VMEM((room, row_width), BF16),
            pltpu.VMEM((depth, wide), BF16),
            pltpu.VMEM((depth, half_width), BF16),
            dma((experts,)),
            dma((experts,)),
            dma((2, GATHER_CHUNKS)),
            dma((2, GATHER_CHUNKS)),
            dma((7, GATHER_CHUNKS)),
            dma((7, GATHER_CHUNKS)),
        ],
        compiler_params=pltpu.CompilerParams(
            collective_id=0, has_side_effects=True, vmem_limit_bytes=VMEM_BYTES
        ),
    )(expert_ids.T, held, swap_pairs, gate_probs, tokens, out_grad, w_in[0], w_down[0])
    part = depth // SUM_CHUNKS
    chunked = (SUM_CHUNKS, part, wide + half_width)
    state_in, state_down = shape((depth, wide), BF16), shape((depth, half_width), BF16)
    result = pl.pallas_call(
        expert_kernel,
        name="expert",
        out_shape=(shape((tok_rows, width), BF16), shape((tok_rows, top_count), F32))
        + (state_in, state_down) * 3,
        in_specs=[vmem, vmem, vmem, smem] + [vmem] * 4,
        out_specs=(vmem,) * 8,
        scratch_shapes=[
            pltpu.VMEM((room, width), BF16),
            pltpu.VMEM((room, wide), BF16),
            pltpu.VMEM((room, half_width), BF16),
            pltpu.VMEM((dp, depth, wide + half_width), BF16),
            pltpu.VMEM((room, width + LANES), BF16),
            pltpu.VMEM((room, width + LANES), BF16),
        ]
        + [pltpu.VMEM(chunked, BF16)] * 8
        + [pltpu.VMEM((depth, wide), BF16), pltpu.VMEM((depth, half_width), BF16)] * 2
        + [dma((experts,))] * 2
        + [dma((4,))] * 2
        + [dma((7, SUM_CHUNKS))] * 2,
        compiler_params=pltpu.CompilerParams(
            collective_id=1, has_side_effects=True, vmem_limit_bytes=VMEM_BYTES
        ),
    )(recv, full, hots, swap_pairs, m_in[0], m_down[0], v_in[0], v_down[0])
    return result[:2] + tuple(r[None] for r in result[2:])


def solution(mesh):
    split = Mesh(mesh.devices.reshape(2, 4, mesh.shape["expert"]), ("dp_0", "dp_1", "expert"))
    rows = P(DP_EXPERT, None)
    state = P("expert", DP, None)
    return jax.shard_map(
        body,
        mesh=split,
        in_specs=(rows,) * 4 + (P(), P()) + (state,) * 6,
        out_specs=(rows, rows) + (state,) * 6,
        check_vma=False,
    )
```

time: 439 us -> 270 us (0.62)
  Pallas kernels: 0 us -> 248 us
  blocking collectives: 153 us -> 0 us
  waiting for transfers between devices: 151 us -> 0 us
  other arithmetic: 30.6 us -> 0.74 us
  matrix products: 28.6 us -> 0 us
  local copies, waits for them, and re-layouts: 37.3 us -> 17.8 us
  starting transfers between devices: 19.4 us -> 0 us
  between operations: 14.1 us -> 0.65 us
    pallas_call x0 -> x2, Pallas kernels: none -> 248 us  [the longest x1 139 us: body(): pl.pallas_call(gather_kernel, name='gather', out_shape=(shape((room, row_...]
    all_to_all x1 -> x0, blocking collectives: 153 us -> none  [side_by_side_2(): lax.all_to_all(both, axis, split_axis=split_dim, concat_axis=concat_dim,...]
    reduce_scatter x4 -> x0, waiting for transfers between devices: 76.6 us -> none  [own_block(): parts = lax.psum_scatter(parts, axes[k], scatter_dimension=0, tiled=True)]
    ppermute x6 -> x0, waiting for transfers between devices: 51.9 us -> none  [passed_along(): lax.ppermute(x, axis, [(i, (i + by) % length) for i in range(length)])]
    dot_general x6 -> x0, matrix products: 28.6 us -> none  [the longest x1 6.47 us: expert_pass(): lax.dot_general(pre_grad, weight_in, (((1,), (1,)), ((), ())), preferred_...]
    all_gather x1 -> x0, waiting for transfers between devices: 22.2 us -> none  [side_by_side(): lax.all_gather(both, axis, axis=dim, tiled=True)]
    gather x4 -> x0, local copies, waits for them, and re-layouts: 14.3 us -> none  [the longest x1 5.24 us: body(): picked_grad = jnp.take(back_grad.reshape(room, -1), buffer_pos, axis=0)]
    unnamed x35 -> x9, local copies, waits for them, and re-layouts: 2.05 us -> 16.3 us
  transfers between devices with their start and end apart: 12 -> 0, of which waited for: 8 -> 0; matrix products, arithmetic and copies ran while one was open for 17% -> 0% of each run, Pallas kernels for 0% -> 0%
where the time goes in v1:
time: 270 us; the launch traced here: 268 us
  Pallas kernels  248 us (92%)
  local copies, waits for them, and re-layouts  17.8 us (7%)
    pallas_call x1, Pallas kernels, body(): pl.pallas_call(gather_kernel, name='gather', out_shape=(shape((room, row_...  139 us
    pallas_call x1, Pallas kernels, body(): pl.pallas_call(expert_kernel, name='expert', out_shape=(shape((tok_rows,...  109 us
    unnamed x9, local copies, waits for them, and re-layouts  16.3 us

profile of v1, /device:TPU:33, one launch (start us, length us, event | category | flops | bytes accessed | tf_op | source)
XLA Modules:
  0.0 267.6 jit_solution(537236664192492258)
XLA Ops:
  0.6 0.8 fusion
  1.4 0.1 add_bitcast_fusion
  1.5 0.7 pad_add_fusion
  2.2 0.7 copy.24.held_ref
  2.9 1.4 copy.25.probs_ref
  4.3 139.4 %gather.1 = (bf16[512,4224]{1,0:T(8,128)(2,1)}, bf16[2048,2304]{1,0:T(8,128)(2,1)}, bf16[2,512,128]{2,1,0:T(8,128)(2,1)}) custom-call(s32[2,128]{1,0:T(2,128)} %bitcast.29, s32[32,2]{1,0:T(8,128)} %copy.24.held_ref, s32[4]{0:T(128)} %pairs_ref.3, f32[128,2]{1,0:T(8,128)} %copy.25.probs_ref, bf16[128,2048]{1,0:T(8,128)(2,1)} %tokens_ref.1, ...), custom_call_target="tpu_custom_call" | custom-call | tf_op jit(solution)/shard_map/gather/pallas_call | solution.py:465
  143.7 109.0 %expert.1 = (bf16[128,2048]{1,0:T(8,128)(2,1)}, f32[128,2]{1,0:T(8,128)}, bf16[256,1536]{1,0:T(8,128)(2,1)}, bf16[256,768]{1,0:T(8,128)(2,1)}, bf16[256,1536]{1,...) custom-call(bf16[512,4224]{1,0:T(8,128)(2,1)} %get-tuple-element.19.recv_ref, ...), custom_call_target="tpu_custom_call" | custom-call | tf_op jit(solution)/shard_map/expert/pallas_call | solution.py:493
  252.8 1.5 copy.26
  254.2 1.9 copy.34
  256.1 2.1 copy.35
  258.2 1.8 copy.36
  259.9 2.1 copy.37
  262.0 1.8 copy.38
  263.8 2.1 copy.39
  265.8 1.8 copy.40

commit v2 on v1

v2 whole, which is shorter than its diff:
```python
import functools

import jax
import jax.numpy as jnp
from jax import lax
from jax.experimental import pallas as pl
from jax.experimental.pallas import tpu as pltpu
from jax.sharding import Mesh
from jax.sharding import PartitionSpec as P

DP = ("dp_0", "dp_1")
EXPERT = ("ex", "ez", "ec")
DP_EXPERT = DP + EXPERT
MESH = pl.DeviceIdType.MESH
BF16, F32 = jnp.bfloat16, jnp.float32

beta_one = 0.9
beta_two = 0.95
learn_rate = 0.01
adam_eps = 1e-08
bias_one = 1.0 - 0.9**10
bias_two = 1.0 - 0.95**10

LANES = 128
GATHER_CHUNKS = 4
SUM_CHUNKS = 4
ADAM_STEPS = 4
VMEM_BYTES = 60 * 1024 * 1024


def in_parts(column):
    high = column.astype(BF16).astype(F32)
    rest = column - high
    middle = rest.astype(BF16).astype(F32)
    return [high, middle, rest - middle]


def in_lanes(columns):
    lane = lax.broadcasted_iota(jnp.int32, (columns[0].shape[0], LANES), 1)
    result = jnp.zeros(lane.shape, F32)
    for n, column in enumerate(columns):
        result = jnp.where(lane == n, column, result)
    return result.astype(BF16)


def from_parts(parts, start=0):
    parts = parts.astype(F32)
    high, middle, low = (parts[:, start + n : start + n + 1] for n in range(3))
    return high + middle + low


def column_of(row, turn=0):
    n = row.shape[1]
    at, lane = (lax.broadcasted_iota(jnp.int32, (n, n), d) for d in (0, 1))
    return jnp.sum(jnp.where(lane == lax.rem(at + turn, n), row, 0.0), axis=1, keepdims=True)


def row_of(column):
    n = column.shape[0]
    at, lane = (lax.broadcasted_iota(jnp.int32, (n, n), d) for d in (0, 1))
    return jnp.sum(jnp.where(lane == at, column, 0.0), axis=0, keepdims=True)


def dot(a, b, contract=(1, 0)):
    dims = (((contract[0],), (contract[1],)), ((), ()))
    return lax.dot_general(a, b, dims, preferred_element_type=F32)


def swapped_here(pairs_ref, me, half_axis):
    mine = lax.rem(me, half_axis)
    flag = (mine == pairs_ref[0]).astype(jnp.int32)
    for j in range(1, pairs_ref.shape[0]):
        flag = jnp.maximum(flag, (mine == pairs_ref[j]).astype(jnp.int32))
    return flag


def choose(flag, moved, kept):
    return jnp.where(jnp.full(kept.shape, flag, jnp.int32) > 0, moved.astype(F32), kept.astype(F32))


def send(source, target, sems, at, device):
    return pltpu.make_async_remote_copy(
        src_ref=source,
        dst_ref=target,
        send_sem=sems[0].at[at],
        recv_sem=sems[1].at[at],
        device_id=device,
        device_id_type=MESH,
    )


class Place:
    def __init__(self):
        self.z, self.y = lax.axis_index("dp_0"), lax.axis_index("dp_1")
        self.layers, self.ring = lax.axis_size("dp_0"), lax.axis_size("dp_1")
        self.cores, self.planes = lax.axis_size("ec"), lax.axis_size("ez")
        self.side = lax.axis_size("ex") * self.cores
        self.experts = self.side * self.planes
        self.own = lax.axis_index("ex") * self.cores + lax.axis_index("ec")
        self.plane = lax.axis_index("ez")
        self.me = (
            lax.axis_index("ex") * self.planes + self.plane
        ) * self.cores + lax.axis_index("ec")
        self.across = {"dp_0": 1 - self.z}
        self.up = {"dp_1": lax.rem(self.y + 1, self.ring)}
        self.down = {"dp_1": lax.rem(self.y + self.ring - 1, self.ring)}

    def member(self, sideways, planes):
        q = (self.own + sideways) % self.side
        z = (self.plane + planes) % self.planes
        return {"ex": q // self.cores, "ez": z, "ec": q % self.cores}

    def partner(self):
        e = (self.me + self.experts // 2) % self.experts
        return {
            "ex": e // (self.planes * self.cores),
            "ez": (e // self.cores) % self.planes,
            "ec": e % self.cores,
        }

    def offset(self, i):
        return (i % 2) * ((i + 1) // 2) + (1 - i % 2) * (self.experts - i // 2)

    def shard(self, layer, step):
        z = (self.z + layer) % self.layers
        return z * self.ring + (self.y + step) % self.ring

    def greet(self):
        barrier = pltpu.get_barrier_semaphore()

        def hello(k, carry):
            device = self.member(k % self.side, k // self.side)
            pl.semaphore_signal(barrier, inc=1, device_id=device, device_id_type=MESH)
            return carry

        lax.fori_loop(1, self.experts, hello, 0)
        for device in (self.across, self.up, self.down):
            pl.semaphore_signal(barrier, inc=1, device_id=device, device_id_type=MESH)
        pl.semaphore_wait(barrier, self.experts - 1 + 3)


def layer_kernel(
    ids_ref, held_ref, pairs_ref, probs_ref, tokens_ref, grads_ref, w_in_ref, w_down_ref,
    m_in_ref, m_down_ref, v_in_ref, v_down_ref,
    total_ref, weight_ref, back, hots_ref, pm_in, pm_down, pv_in, pv_down,
    tok, send_ref, recv, full_ref, swap_in, swap_down, scaled, pre, hidden, grad, ret,
    on_up, on_down, a_low, a_high, b_low, b_high, z_in,
    tok_send, tok_recv, row_send, row_recv, back_send, back_recv, swap_send, swap_recv,
    moment_send, moment_recv, gather_send, gather_recv, ring_send, ring_recv,
):
    at = Place()
    experts, half_axis = at.experts, at.experts // 2
    tok_rows, width = tokens_ref.shape
    room, row_width = recv.shape
    capacity = room // experts
    plane_room = room // at.planes
    depth, wide = w_in_ref.shape
    half_width = w_down_ref.shape[1]
    at.greet()

    part = depth // GATHER_CHUNKS
    partner = at.partner()
    sems = (swap_send, swap_recv)
    swaps = []
    for c in range(GATHER_CHUNKS):
        rows = pl.ds(c * part, part)
        swaps.append(
            (
                send(w_in_ref.at[rows], swap_in.at[rows], sems, (0, c), partner),
                send(w_down_ref.at[rows], swap_down.at[rows], sems, (1, c), partner),
            )
        )
        for copy in swaps[-1]:
            copy.start()

    slot = lax.broadcasted_iota(jnp.int32, (1, experts), 1)
    flag = (lax.rem(slot, half_axis) == pairs_ref[0]).astype(jnp.int32)
    for j in range(1, pairs_ref.shape[0]):
        flag = jnp.maximum(flag, (lax.rem(slot, half_axis) == pairs_ref[j]).astype(jnp.int32))
    before_swap = held_ref[...].astype(F32)
    held = jnp.where(flag > 0, row_of(column_of(before_swap, half_axis)), before_swap)
    top_count = ids_ref.shape[0]
    hits = [
        (column_of(ids_ref[k : k + 1, :].astype(F32)) == held).astype(F32)
        for k in range(top_count)
    ]
    named = hits[0]
    for hit in hits[1:]:
        named = named + hit
    row, column = (lax.broadcasted_iota(jnp.int32, (tok_rows, tok_rows), d) for d in (0, 1))
    before = dot((column < row).astype(F32).astype(BF16), named.astype(BF16))
    in_plane = lax.div(slot, at.planes * at.cores) * at.cores + lax.rem(slot, at.cores)
    planes_on = lax.rem(lax.rem(lax.div(slot, at.cores), at.planes) + at.planes - at.plane, at.planes)
    sideways = lax.rem(in_plane + at.side - at.own, at.side)
    first = ((planes_on * at.side + sideways) * capacity).astype(F32)
    room_ids = lax.broadcasted_iota(jnp.int32, (tok_rows, room), 1)
    columns = []
    for k in range(top_count):
        columns += in_parts(column_of(probs_ref[k : k + 1, :]))
    for k, hit in enumerate(hits):
        place = jnp.sum(hit * (before + first), axis=1, keepdims=True).astype(jnp.int32)
        hots_ref[k] = (room_ids == place).astype(F32).astype(BF16)
        high = lax.div(place, capacity)
        columns += [high.astype(F32), (place - high * capacity).astype(F32)]
    tok[0, :, pl.ds(2 * width, LANES)] = in_lanes(columns)
    tok[0, :, pl.ds(0, width)] = tokens_ref[...]
    tok[0, :, pl.ds(width, width)] = grads_ref[...]

    half_rows = tok_rows // 2
    tok_sems = (tok_send, tok_recv)

    def block(d, h):
        return tok.at[d, pl.ds(h * half_rows, half_rows)]

    def to_plane(kind, h):
        up = at.member(0, 1)
        down = at.member(0, at.planes - 1)
        if kind == 2:
            source, device = (block(1, 0), up) if h == 0 else (block(3, 1), down)
            return send(source, block(2, h), tok_sems, (2, h), device)
        target = block(1, h) if kind == 0 else block(3, h)
        return send(block(0, h), target, tok_sems, (kind, h), up if kind == 0 else down)

    to_plane(0, 0).start()
    to_plane(1, 1).start()

    def row_copy(d, r):
        rows = pl.ds(pl.multiple_of(d * plane_room + r * capacity, capacity), capacity)
        n = d * at.side + r
        return send(
            send_ref.at[rows], recv.at[rows], (row_send, row_recv), n, at.member(r, 0)
        )

    def dispatch(d):
        lanes = tok[d, :, pl.ds(2 * width, LANES)]
        slots = lax.broadcasted_iota(jnp.int32, (tok_rows, plane_room), 1) + d * plane_room
        lane = lax.broadcasted_iota(jnp.int32, lanes.shape, 1)
        number = lanes.astype(F32)
        both = jnp.zeros((plane_room, tok_rows), F32)
        parts = jnp.zeros((plane_room, LANES), F32)
        for k in range(top_count):
            start = 3 * top_count + 2 * k
            place = number[:, start : start + 1] * capacity + number[:, start + 1 : start + 2]
            hot = (slots == place.astype(jnp.int32)).astype(F32).T
            both = both + hot
            own = jnp.where(lane >= 3 * k, jnp.where(lane < 3 * k + 3, number, 0.0), 0.0)
            parts = parts + dot(hot.astype(BF16), own.astype(BF16))
        rows = pl.ds(d * plane_room, plane_room)
        both = both.astype(BF16)
        step = min(512, width)
        for c in range(2 * width // step):
            columns = pl.ds(c * step, step)
            send_ref[rows, columns] = dot(both, tok[d, :, columns]).astype(BF16)
        send_ref[rows, pl.ds(2 * width, LANES)] = parts.astype(BF16)

        def start_row(r, carry):
            row_copy(d, r).start()
            return carry

        lax.fori_loop(1, at.side, start_row, 0)
        own_rows = pl.ds(d * plane_room, capacity)
        recv[own_rows] = send_ref[own_rows]

    dispatch(0)

    flag = swapped_here(pairs_ref, at.me, half_axis)
    gather = (gather_send, gather_recv)

    def shard(layer, step, c):
        start = at.shard(layer, step) * depth + c * part
        return full_ref.at[pl.ds(pl.multiple_of(start, part), part)]

    def spread(kind, layer, step, c, device):
        shared = shard(layer, step, c)
        return send(shared, shared, gather, (kind, c), device)

    spreading = []

    def begin_spread(*what):
        copy = spread(*what)
        copy.start()
        spreading.append(copy)

    ACROSS, UP_OWN, DOWN_OWN, UP_OTHER, DOWN_OTHER, UP_ON, DOWN_ON = range(7)

    def open_gather(c):
        for copy in swaps[c]:
            copy.wait_recv()
        rows = pl.ds(c * part, part)
        mine = shard(0, 0, c)
        new_in = choose(flag, swap_in[rows], w_in_ref[rows]).astype(BF16)
        new_down = choose(flag, swap_down[rows], w_down_ref[rows]).astype(BF16)
        mine[:, pl.ds(0, wide)] = new_in
        mine[:, pl.ds(wide, half_width)] = new_down
        weight_ref[rows, pl.ds(0, wide)] = new_in
        weight_ref[rows, pl.ds(wide, half_width)] = new_down
        begin_spread(ACROSS, 0, 0, c, at.across)
        begin_spread(UP_OWN, 0, 0, c, at.up)
        begin_spread(DOWN_OWN, 0, 0, c, at.down)

    def pass_own(c):
        spread(UP_OWN, 0, -1, c, at.up).wait_recv()
        begin_spread(UP_ON, 0, -1, c, at.up)

    def spread_other(c):
        spread(ACROSS, 1, 0, c, at.across).wait_recv()
        begin_spread(UP_OTHER, 1, 0, c, at.up)
        begin_spread(DOWN_OTHER, 1, 0, c, at.down)

    def pass_other(c):
        spread(DOWN_OTHER, 1, 1, c, at.down).wait_recv()
        begin_spread(DOWN_ON, 1, 1, c, at.down)

    chunks = range(GATHER_CHUNKS)
    middle = GATHER_CHUNKS // 2
    for c in chunks:
        open_gather(c)
    to_plane(0, 1).start()
    to_plane(1, 0).start()
    for c in chunks[:middle]:
        pass_own(c)
    to_plane(0, 0).wait_recv()
    to_plane(2, 0).start()
    to_plane(1, 1).wait_recv()
    to_plane(2, 1).start()
    for c in chunks[:middle]:
        spread_other(c)
    for c in chunks[middle:]:
        pass_own(c)
    for c in chunks[middle:]:
        spread_other(c)
    to_plane(0, 1).wait_recv()
    dispatch(1)
    for c in chunks[:middle]:
        pass_other(c)
    to_plane(1, 0).wait_recv()
    dispatch(3)
    for c in chunks[middle:]:
        pass_other(c)
    to_plane(2, 0).wait_recv()
    to_plane(2, 1).wait_recv()
    dispatch(2)

    moments = []
    for n, (own, other) in enumerate(
        ((m_in_ref, pm_in), (m_down_ref, pm_down), (v_in_ref, pv_in), (v_down_ref, pv_down))
    ):
        moments.append(send(own, other, (moment_send, moment_recv), n, partner))
        moments[-1].start()

    for c in chunks:
        spread(DOWN_OWN, 0, 1, c, at.down).wait_recv()
        spread(UP_OTHER, 1, -1, c, at.up).wait_recv()
        spread(UP_ON, 0, -2, c, at.up).wait_recv()
        spread(DOWN_ON, 1, 2, c, at.down).wait_recv()

    def wait_plane(d, carry):
        def wait_row(r, carry):
            row_copy(d, r).wait_recv()
            return carry

        return lax.fori_loop(1, at.side, wait_row, carry)

    lax.fori_loop(0, at.planes, wait_plane, 0)

    lanes = recv[:, 2 * width :]
    rows_p = from_parts(lanes)
    for k in range(1, top_count):
        rows_p = rows_p + from_parts(lanes, 3 * k)
    step = min(512, width)
    for c in range(width // step):
        columns = pl.ds(c * step, step)
        rows_g = recv[:, pl.ds(width + c * step, step)].astype(F32)
        scaled[:, columns] = (rows_p * rows_g).astype(BF16)
    span = min(256, half_width)

    def through(n, carry):
        gate_at = pl.multiple_of(n * span, span)
        up_at = pl.multiple_of(half_width + n * span, span)
        down_at = pl.multiple_of(wide + n * span, span)
        gate_part = dot(recv[:, :width], full_ref[:, pl.ds(gate_at, span)])
        up_part = dot(recv[:, :width], full_ref[:, pl.ds(up_at, span)])
        hidden_grad = dot(scaled[...], full_ref[:, pl.ds(down_at, span)])
        sigmoid = jax.nn.sigmoid(gate_part)
        activated = gate_part * sigmoid
        slope_term = sigmoid * (1.0 + gate_part * (1.0 - sigmoid))
        hidden[:, pl.ds(gate_at, span)] = (activated * up_part).astype(BF16)
        pre[:, pl.ds(gate_at, span)] = (hidden_grad * up_part * slope_term).astype(BF16)
        pre[:, pl.ds(up_at, span)] = (hidden_grad * activated).astype(BF16)
        return carry

    lax.fori_loop(0, half_width // span, through, 0)

    def weight_grads(i, carry):
        start = pl.multiple_of(at.shard(i % 2, 2 + i // 2) * depth, depth)
        columns = pl.ds(start, depth)
        grad[i, :, pl.ds(0, wide)] = dot(recv[:, columns], pre[...], (0, 0)).astype(BF16)
        grad[i, :, pl.ds(wide, half_width)] = dot(
            scaled[:, columns], hidden[...], (0, 0)
        ).astype(BF16)
        return carry

    ring = (ring_send, ring_recv)
    summing = []
    part = depth // SUM_CHUNKS

    def begin(source, target, kind, c, device):
        copy = send(source, target.at[c], ring, (kind, c), device)
        copy.start()
        summing.append(copy)

    def arrived(target, kind, c):
        send(target.at[c], target.at[c], ring, (kind, c), at.up).wait_recv()
        return target[c].astype(F32)

    def rows_of(c):
        return pl.ds(c * part, part)

    A2, B2, A3, B3, A0, B0, A1, B1 = range(8)
    ON_UP, ON_DOWN, A_LOW, A_HIGH, B_LOW, B_HIGH, Z = range(7)
    lax.fori_loop(0, 2, weight_grads, 0)
    for c in range(SUM_CHUNKS):
        begin(grad.at[A2, rows_of(c)], on_up, ON_UP, c, at.up)
        begin(grad.at[B2, rows_of(c)], on_down, ON_DOWN, c, at.down)
    lax.fori_loop(2, 8, weight_grads, 0)
    early = SUM_CHUNKS // 2
    for c in range(early):
        begin(grad.at[B1, rows_of(c)], b_low, B_LOW, c, at.up)
        begin(grad.at[A3, rows_of(c)], a_high, A_HIGH, c, at.down)

    span_out = min(256, width)

    def row_grads(n, total):
        start = pl.multiple_of(n * span_out, span_out)
        rows = pl.ds(start, span_out)
        ret[:, rows] = dot(pre[...], full_ref[rows, pl.ds(0, wide)], (1, 1)).astype(BF16)
        out = dot(hidden[...], full_ref[rows, pl.ds(wide, half_width)], (1, 1)).astype(BF16)
        rows_g = recv[:, pl.ds(pl.multiple_of(width + start, span_out), span_out)].astype(F32)
        return total + jnp.sum(out.astype(F32) * rows_g, axis=1, keepdims=True)

    row_total = lax.fori_loop(0, width // span_out, row_grads, jnp.zeros((room, 1), F32))
    ret[:, width:] = in_lanes(in_parts(row_total))

    def rows_to(i):
        k = at.offset(i)
        rows = pl.ds(pl.multiple_of(k * capacity, capacity), capacity)
        device = at.member(at.side - k % at.side, at.planes - k // at.side)
        return send(ret.at[rows], back.at[rows], (back_send, back_recv), k, device)

    def start_rows(i, carry):
        rows_to(i).start()
        return carry

    def wait_rows(i, carry):
        rows_to(i).wait()
        return carry

    lax.fori_loop(1, experts, start_rows, 0)
    back[0:capacity] = ret[0:capacity]

    def pass_on(c):
        low = grad[A1, rows_of(c)].astype(F32) + arrived(on_up, ON_UP, c)
        grad[A1, rows_of(c)] = low.astype(BF16)
        begin(grad.at[A1, rows_of(c)], a_low, A_LOW, c, at.up)
        high = grad[B3, rows_of(c)].astype(F32) + arrived(on_down, ON_DOWN, c)
        grad[B3, rows_of(c)] = high.astype(BF16)
        begin(grad.at[B3, rows_of(c)], b_high, B_HIGH, c, at.down)

    for c in range(SUM_CHUNKS):
        pass_on(c)
        if c + early < SUM_CHUNKS:
            begin(grad.at[B1, rows_of(c + early)], b_low, B_LOW, c + early, at.up)
            begin(grad.at[A3, rows_of(c + early)], a_high, A_HIGH, c + early, at.down)

    def hand_over(c):
        mine = grad[B0, rows_of(c)].astype(F32)
        mine = mine + arrived(b_low, B_LOW, c) + arrived(b_high, B_HIGH, c)
        grad[B0, rows_of(c)] = mine.astype(BF16)
        begin(grad.at[B0, rows_of(c)], z_in, Z, c, at.across)

    def add_up(c):
        mine = grad[A0, rows_of(c)].astype(F32)
        mine = mine + arrived(a_low, A_LOW, c) + arrived(a_high, A_HIGH, c)
        total_ref[rows_of(c)] = mine + arrived(z_in, Z, c)

    for c in range(SUM_CHUNKS):
        hand_over(c)
        if c > 0:
            add_up(c - 1)
    add_up(SUM_CHUNKS - 1)
    lax.fori_loop(1, experts, wait_rows, 0)
    for copy in moments:
        copy.wait()

    def wait_sent(d, carry):
        def wait_row(r, carry):
            row_copy(d, r).wait_send()
            return carry

        return lax.fori_loop(1, at.side, wait_row, carry)

    lax.fori_loop(0, at.planes, wait_sent, 0)
    for kind in range(3):
        for h in range(2):
            to_plane(kind, h).wait_send()
    for pair in swaps:
        for copy in pair:
            copy.wait_send()
    for copy in spreading + summing:
        copy.wait_send()


def update_kernel(
    pairs_ref, total_ref, weight_ref, back, back_lanes, hots_ref,
    m_in_ref, m_down_ref, v_in_ref, v_down_ref, pm_in, pm_down, pv_in, pv_down,
    token_ref, prob_ref, nw_in, nw_down, nm_in, nm_down, nv_in, nv_down,
):
    at = Place()
    flag = swapped_here(pairs_ref, at.me, at.experts // 2)
    wide, half_width = m_in_ref.shape[1], m_down_ref.shape[1]
    for start, size, refs in (
        (0, wide, (pm_in, m_in_ref, pv_in, v_in_ref, nw_in, nm_in, nv_in)),
        (wide, half_width, (pm_down, m_down_ref, pv_down, v_down_ref, nw_down, nm_down, nv_down)),
    ):
        columns = pl.ds(start, size)
        value = total_ref[:, columns]
        first = choose(flag, refs[0][...], refs[1][...])
        second = choose(flag, refs[2][...], refs[3][...])
        weight = weight_ref[:, columns].astype(F32)
        first_new = beta_one * first + (1.0 - beta_one) * value
        second_new = beta_two * second + (1.0 - beta_two) * value * value
        step_size = first_new / bias_one / (jnp.sqrt(second_new / bias_two) + adam_eps)
        refs[4][...] = (weight - learn_rate * step_size).astype(BF16)
        refs[5][...] = first_new.astype(BF16)
        refs[6][...] = second_new.astype(BF16)
    hots = [hots_ref[k] for k in range(hots_ref.shape[0])]
    both = hots[0]
    for hot in hots[1:]:
        both = both + hot
    token_ref[...] = dot(both, back[...]).astype(BF16)

    @pl.when(pl.program_id(0) == 0)
    def _():
        for k, hot in enumerate(hots):
            prob_ref[:, k : k + 1] = from_parts(dot(hot, back_lanes[...]))


def body(
    tokens,
    out_grad,
    expert_ids,
    gate_probs,
    held_expert,
    swap_pairs,
    w_in,
    w_down,
    m_in,
    m_down,
    v_in,
    v_down,
):
    experts = lax.axis_size(EXPERT)
    planes, side = lax.axis_size("ez"), experts // lax.axis_size("ez")
    dp = lax.axis_size(DP)
    tok_rows, width = tokens.shape
    top_count = expert_ids.shape[1]
    capacity = max(2, 2 * tok_rows * top_count // experts)
    room = experts * capacity
    _, depth, wide = w_in.shape
    half_width = w_down.shape[2]
    joint = wide + half_width
    row_width = 2 * width + LANES
    vmem = pl.BlockSpec(memory_space=pltpu.VMEM)
    smem = pl.BlockSpec(memory_space=pltpu.SMEM)
    anywhere = pl.BlockSpec(memory_space=pl.ANY)
    dma = pltpu.SemaphoreType.DMA
    shape = jax.ShapeDtypeStruct
    chunked = pltpu.VMEM((SUM_CHUNKS, depth // SUM_CHUNKS, joint), BF16)
    state_in, state_down = shape((depth, wide), BF16), shape((depth, half_width), BF16)
    moments = (m_in[0], m_down[0], v_in[0], v_down[0])
    total, weight, back, hots, *moved = pl.pallas_call(
        layer_kernel,
        name="layer",
        out_shape=(
            shape((depth, joint), F32),
            shape((depth, joint), BF16),
            shape((room, width + LANES), BF16),
            shape((top_count, tok_rows, room), BF16),
        )
        + (state_in, state_down) * 2,
        in_specs=[vmem, vmem, smem] + [vmem] * 5 + [anywhere] * 4,
        out_specs=(vmem,) * 4 + (anywhere,) * 4,
        scratch_shapes=[
            pltpu.VMEM((planes, tok_rows, row_width), BF16),
            pltpu.VMEM((room, row_width), BF16),
            pltpu.VMEM((room, row_width), BF16),
            pltpu.VMEM((dp * depth, joint), BF16),
            pltpu.VMEM((depth, wide), BF16),
            pltpu.VMEM((depth, half_width), BF16),
            pltpu.VMEM((room, width), BF16),
            pltpu.VMEM((room, wide), BF16),
            pltpu.VMEM((room, half_width), BF16),
            pltpu.VMEM((dp, depth, joint), BF16),
            pltpu.VMEM((room, width + LANES), BF16),
        ]
        + [chunked] * 7
        + [dma((3, 2))] * 2
        + [dma((experts,))] * 4
        + [dma((2, GATHER_CHUNKS))] * 2
        + [dma((4,))] * 2
        + [dma((7, GATHER_CHUNKS))] * 2
        + [dma((7, SUM_CHUNKS))] * 2,
        compiler_params=pltpu.CompilerParams(
            collective_id=0, has_side_effects=True, vmem_limit_bytes=VMEM_BYTES
        ),
    )(
        expert_ids.T,
        held_expert.reshape(1, experts),
        swap_pairs,
        gate_probs.T,
        tokens,
        out_grad,
        w_in[0],
        w_down[0],
        *moments,
    )
    steps = ADAM_STEPS

    def rows(columns):
        return pl.BlockSpec((depth // steps, columns), lambda i: (i, 0))

    states = [rows(wide), rows(half_width)]
    result = pl.pallas_call(
        update_kernel,
        name="update",
        grid=(steps,),
        out_shape=(shape((tok_rows, width), BF16), shape((tok_rows, top_count), F32))
        + (state_in, state_down) * 3,
        in_specs=[
            smem,
            rows(joint),
            rows(joint),
            pl.BlockSpec((room, width // steps), lambda i: (0, i)),
            pl.BlockSpec((room, LANES), lambda i: (0, width // LANES)),
            pl.BlockSpec((top_count, tok_rows, room), lambda i: (0, 0, 0)),
        ]
        + states * 4,
        out_specs=[
            pl.BlockSpec((tok_rows, width // steps), lambda i: (0, i)),
            pl.BlockSpec((tok_rows, top_count), lambda i: (0, 0)),
        ]
        + states * 3,
    )(swap_pairs, total, weight, back, back, hots, *moments, *moved)
    return tuple(result[:2]) + tuple(r[None] for r in result[2:])


def solution(mesh):
    experts = mesh.shape["expert"]
    shape = (2, 4, experts // 8, 4, 2)
    split = Mesh(mesh.devices.reshape(shape), DP_EXPERT)
    rows = P(DP_EXPERT, None)
    state = P(EXPERT, DP, None)
    return jax.shard_map(
        body,
        mesh=split,
        in_specs=(rows,) * 4 + (P(), P()) + (state,) * 6,
        out_specs=(rows, rows) + (state,) * 6,
        check_vma=False,
    )
```

time: 270 us -> 243 us (0.900)
  local copies, waits for them, and re-layouts: 17.8 us -> 1.48 us
  Pallas kernels: 248 us -> 241 us
    unnamed x9 -> x1, local copies, waits for them, and re-layouts: 16.3 us -> 1.48 us
    pallas_call x2, Pallas kernels: 248 us -> 241 us  [the longest x1 232 us: body(): pl.pallas_call(layer_kernel, name='layer', out_shape=(shape((depth, joint...]
where the time goes in v2:
time: 243 us
  Pallas kernels  241 us (99%)
    pallas_call x1, Pallas kernels, body(): pl.pallas_call(layer_kernel, name='layer', out_shape=(shape((depth, joint...  232 us
    pallas_call x1, Pallas kernels, body(): pl.pallas_call(update_kernel, name='update', grid=(steps,), out_shape=(sh...  8.8 us

profile of v2, /device:TPU:33, one launch (start us, length us, event | category | flops | bytes accessed | tf_op | source)
XLA Modules:
  0.0 243.1 jit_solution(8375745727543202559)
XLA Ops:
  0.6 232.2 %layer.1 = (f32[256,2304]{1,0:T(8,128)}, bf16[256,2304]{1,0:T(8,128)(2,1)}, bf16[512,2176]{1,0:T(8,128)(2,1)}, bf16[2,128,512]{2,1,0:T(8,128)(2,1)}, bf16[256,15...) custom-call(s32[2,128]{1,0:T(2,128)} %bitcast.25, ...), custom_call_target="tpu_custom_call" | custom-call | tf_op jit(solution)/shard_map/layer/pallas_call | solution.py:581
  232.8 8.8 %update.1 = (bf16[128,2048]{1,0:T(8,128)(2,1)}, f32[128,2]{1,0:T(8,128)}, bf16[256,1536]{1,0:T(8,128)(2,1)}, bf16[256,768]{1,0:T(8,128)(2,1)}, bf16[256,1536]{1,...) custom-call(s32[4]{0:T(128)} %pairs_ref.3, ...), custom_call_target="tpu_custom_call" | custom-call | tf_op jit(solution)/shard_map/update/pallas_call | solution.py:633
  241.6 1.5 copy.20

commit v3 on v2

--- a/solution.py
+++ b/solution.py
@@ -22,8 +22,8 @@
 bias_two = 1.0 - 0.95**10
 
 LANES = 128
-GATHER_CHUNKS = 4
-SUM_CHUNKS = 4
+PART_UNITS = 256
+HALVES = 2
 ADAM_STEPS = 4
 VMEM_BYTES = 60 * 1024 * 1024
 
@@ -143,7 +143,7 @@
     ids_ref, held_ref, pairs_ref, probs_ref, tokens_ref, grads_ref, w_in_ref, w_down_ref,
     m_in_ref, m_down_ref, v_in_ref, v_down_ref,
     total_ref, weight_ref, back, hots_ref, pm_in, pm_down, pv_in, pv_down,
-    tok, send_ref, recv, full_ref, swap_in, swap_down, scaled, pre, hidden, grad, ret,
+    tok, send_ref, recv, full_ref, swap_in, swap_down, scaled, x_turned, s_turned, pre, hidden, grad,
     on_up, on_down, a_low, a_high, b_low, b_high, z_in,
     tok_send, tok_recv, row_send, row_recv, back_send, back_recv, swap_send, swap_recv,
     moment_send, moment_recv, gather_send, gather_recv, ring_send, ring_recv,
@@ -158,16 +158,40 @@
     half_width = w_down_ref.shape[1]
     at.greet()
 
-    part = depth // GATHER_CHUNKS
+    half_rows = tok_rows // 2
+    tok_sems = (tok_send, tok_recv)
+    plane_up, plane_down = at.member(0, 1), at.member(0, at.planes - 1)
+    pieces = (pl.ds(0, width), pl.ds(width, width), pl.ds(2 * width, LANES))
+
+    def block(d, h, piece):
+        return tok.at[d, pl.ds(h * half_rows, half_rows), pieces[piece]]
+
+    def to_plane(kind, h, piece):
+        if kind == 2:
+            source, device = (block(1, 0, piece), plane_up) if h == 0 else (block(3, 1, piece), plane_down)
+            target = block(2, h, piece)
+        else:
+            rows = pl.ds(h * half_rows, half_rows)
+            source = (tokens_ref.at[rows], grads_ref.at[rows], block(0, h, piece))[piece]
+            target, device = (block(1, h, piece), plane_up) if kind == 0 else (block(3, h, piece), plane_down)
+        return send(source, target, tok_sems, (kind, h, piece), device)
+
+    for piece in range(2):
+        to_plane(0, 0, piece).start()
+        to_plane(1, 1, piece).start()
+
+    span = min(PART_UNITS, half_width)
+    parts = half_width // span
     partner = at.partner()
     sems = (swap_send, swap_recv)
     swaps = []
-    for c in range(GATHER_CHUNKS):
-        rows = pl.ds(c * part, part)
+    for c in range(parts):
+        gate, up = pl.ds(c * span, span), pl.ds(half_width + c * span, span)
         swaps.append(
             (
-                send(w_in_ref.at[rows], swap_in.at[rows], sems, (0, c), partner),
-                send(w_down_ref.at[rows], swap_down.at[rows], sems, (1, c), partner),
+                send(w_in_ref.at[:, gate], swap_in.at[:, gate], sems, (0, c), partner),
+                send(w_in_ref.at[:, up], swap_in.at[:, up], sems, (1, c), partner),
+                send(w_down_ref.at[:, gate], swap_down.at[:, gate], sems, (2, c), partner),
             )
         )
         for copy in swaps[-1]:
@@ -203,26 +227,8 @@
         high = lax.div(place, capacity)
         columns += [high.astype(F32), (place - high * capacity).astype(F32)]
     tok[0, :, pl.ds(2 * width, LANES)] = in_lanes(columns)
-    tok[0, :, pl.ds(0, width)] = tokens_ref[...]
-    tok[0, :, pl.ds(width, width)] = grads_ref[...]
-
-    half_rows = tok_rows // 2
-    tok_sems = (tok_send, tok_recv)
-
-    def block(d, h):
-        return tok.at[d, pl.ds(h * half_rows, half_rows)]
-
-    def to_plane(kind, h):
-        up = at.member(0, 1)
-        down = at.member(0, at.planes - 1)
-        if kind == 2:
-            source, device = (block(1, 0), up) if h == 0 else (block(3, 1), down)
-            return send(source, block(2, h), tok_sems, (2, h), device)
-        target = block(1, h) if kind == 0 else block(3, h)
-        return send(block(0, h), target, tok_sems, (kind, h), up if kind == 0 else down)
-
-    to_plane(0, 0).start()
-    to_plane(1, 1).start()
+    to_plane(0, 0, 2).start()
+    to_plane(1, 1, 2).start()
 
     def row_copy(d, r):
         rows = pl.ds(pl.multiple_of(d * plane_room + r * capacity, capacity), capacity)
@@ -237,21 +243,27 @@
         lane = lax.broadcasted_iota(jnp.int32, lanes.shape, 1)
         number = lanes.astype(F32)
         both = jnp.zeros((plane_room, tok_rows), F32)
-        parts = jnp.zeros((plane_room, LANES), F32)
+        values = jnp.zeros((plane_room, LANES), F32)
         for k in range(top_count):
             start = 3 * top_count + 2 * k
             place = number[:, start : start + 1] * capacity + number[:, start + 1 : start + 2]
             hot = (slots == place.astype(jnp.int32)).astype(F32).T
             both = both + hot
             own = jnp.where(lane >= 3 * k, jnp.where(lane < 3 * k + 3, number, 0.0), 0.0)
-            parts = parts + dot(hot.astype(BF16), own.astype(BF16))
+            values = values + dot(hot.astype(BF16), own.astype(BF16))
         rows = pl.ds(d * plane_room, plane_room)
         both = both.astype(BF16)
         step = min(512, width)
         for c in range(2 * width // step):
             columns = pl.ds(c * step, step)
-            send_ref[rows, columns] = dot(both, tok[d, :, columns]).astype(BF16)
-        send_ref[rows, pl.ds(2 * width, LANES)] = parts.astype(BF16)
+            if d > 0:
+                source = tok[d, :, columns]
+            elif c * step < width:
+                source = tokens_ref[:, columns]
+            else:
+                source = grads_ref[:, pl.ds(c * step - width, step)]
+            send_ref[rows, columns] = dot(both, source).astype(BF16)
+        send_ref[rows, pl.ds(2 * width, LANES)] = values.astype(BF16)
 
         def start_row(r, carry):
             row_copy(d, r).start()
@@ -261,14 +273,34 @@
         own_rows = pl.ds(d * plane_room, capacity)
         recv[own_rows] = send_ref[own_rows]
 
+    def take_rows(d):
+        def wait_row(r, carry):
+            row_copy(d, r).wait_recv()
+            return carry
+
+        lax.fori_loop(1, at.side, wait_row, 0)
+        rows = pl.ds(d * plane_room, plane_room)
+        lanes = recv[rows, pl.ds(2 * width, LANES)]
+        rows_p = from_parts(lanes)
+        for k in range(1, top_count):
+            rows_p = rows_p + from_parts(lanes, 3 * k)
+        step = min(512, width)
+        for c in range(width // step):
+            columns = pl.ds(c * step, step)
+            rows_g = recv[rows, pl.ds(width + c * step, step)].astype(F32)
+            rows_s = (rows_p * rows_g).astype(BF16)
+            scaled[rows, columns] = rows_s
+            s_turned[columns, rows] = rows_s.T
+            x_turned[columns, rows] = recv[rows, columns].T
+
     dispatch(0)
 
     flag = swapped_here(pairs_ref, at.me, half_axis)
     gather = (gather_send, gather_recv)
 
     def shard(layer, step, c):
-        start = at.shard(layer, step) * depth + c * part
-        return full_ref.at[pl.ds(pl.multiple_of(start, part), part)]
+        start = at.shard(layer, step) * depth
+        return full_ref.at[c, pl.ds(pl.multiple_of(start, depth), depth)]
 
     def spread(kind, layer, step, c, device):
         shared = shard(layer, step, c)
@@ -286,17 +318,19 @@
     def open_gather(c):
         for copy in swaps[c]:
             copy.wait_recv()
-        rows = pl.ds(c * part, part)
         mine = shard(0, 0, c)
-        new_in = choose(flag, swap_in[rows], w_in_ref[rows]).astype(BF16)
-        new_down = choose(flag, swap_down[rows], w_down_ref[rows]).astype(BF16)
-        mine[:, pl.ds(0, wide)] = new_in
-        mine[:, pl.ds(wide, half_width)] = new_down
-        weight_ref[rows, pl.ds(0, wide)] = new_in
-        weight_ref[rows, pl.ds(wide, half_width)] = new_down
-        begin_spread(ACROSS, 0, 0, c, at.across)
+        for n, (here, there, start) in enumerate(
+            ((w_in_ref, swap_in, 0), (w_in_ref, swap_in, half_width), (w_down_ref, swap_down, 0))
+        ):
+            columns = pl.ds(start + c * span, span)
+            new = choose(flag, there[:, columns], here[:, columns]).astype(BF16)
+            mine[:, pl.ds(n * span, span)] = new
+            weight_ref[:, pl.ds(n * half_width + c * span, span)] = new
         begin_spread(UP_OWN, 0, 0, c, at.up)
         begin_spread(DOWN_OWN, 0, 0, c, at.down)
+
+    def cross(c):
+        begin_spread(ACROSS, 0, 0, c, at.across)
 
     def pass_own(c):
         spread(UP_OWN, 0, -1, c, at.up).wait_recv()
@@ -311,98 +345,65 @@
         spread(DOWN_OTHER, 1, 1, c, at.down).wait_recv()
         begin_spread(DOWN_ON, 1, 1, c, at.down)
 
-    chunks = range(GATHER_CHUNKS)
-    middle = GATHER_CHUNKS // 2
-    for c in chunks:
+    every = range(parts)
+
+    def more_blocks():
+        for piece in range(3):
+            to_plane(0, 1, piece).start()
+            to_plane(1, 0, piece).start()
+
+    def pass_blocks():
+        for kind, h in ((0, 0), (1, 1)):
+            for piece in range(3):
+                to_plane(kind, h, piece).wait_recv()
+            for piece in range(3):
+                to_plane(2, h, piece).start()
+
+    def spread_block(d):
+        for kind, h in {1: ((0, 1),), 3: ((1, 0),), 2: ((2, 0), (2, 1))}[d]:
+            for piece in range(3):
+                to_plane(kind, h, piece).wait_recv()
+        dispatch(d)
+
+    pairs_of = ((m_in_ref, pm_in), (m_down_ref, pm_down), (v_in_ref, pv_in), (v_down_ref, pv_down))
+    moments = [
+        send(own, other, (moment_send, moment_recv), n, partner)
+        for n, (own, other) in enumerate(pairs_of)
+    ]
+    for c in every:
         open_gather(c)
-    to_plane(0, 1).start()
-    to_plane(1, 0).start()
-    for c in chunks[:middle]:
+        cross(c)
+    more_blocks()
+    for c in every[:-1]:
         pass_own(c)
-    to_plane(0, 0).wait_recv()
-    to_plane(2, 0).start()
-    to_plane(1, 1).wait_recv()
-    to_plane(2, 1).start()
-    for c in chunks[:middle]:
+    pass_blocks()
+    for c in every[:-1]:
         spread_other(c)
-    for c in chunks[middle:]:
-        pass_own(c)
-    for c in chunks[middle:]:
-        spread_other(c)
-    to_plane(0, 1).wait_recv()
-    dispatch(1)
-    for c in chunks[:middle]:
+    pass_own(parts - 1)
+    spread_other(parts - 1)
+    spread_block(1)
+    pass_other(0)
+    spread_block(3)
+    for c in every[1:]:
         pass_other(c)
-    to_plane(1, 0).wait_recv()
-    dispatch(3)
-    for c in chunks[middle:]:
-        pass_other(c)
-    to_plane(2, 0).wait_recv()
-    to_plane(2, 1).wait_recv()
-    dispatch(2)
-
-    moments = []
-    for n, (own, other) in enumerate(
-        ((m_in_ref, pm_in), (m_down_ref, pm_down), (v_in_ref, pv_in), (v_down_ref, pv_down))
-    ):
-        moments.append(send(own, other, (moment_send, moment_recv), n, partner))
-        moments[-1].start()
-
-    for c in chunks:
+    spread_block(2)
+    for copy in moments[:2]:
+        copy.start()
+
+    def gathered(c):
         spread(DOWN_OWN, 0, 1, c, at.down).wait_recv()
         spread(UP_OTHER, 1, -1, c, at.up).wait_recv()
         spread(UP_ON, 0, -2, c, at.up).wait_recv()
         spread(DOWN_ON, 1, 2, c, at.down).wait_recv()
 
-    def wait_plane(d, carry):
-        def wait_row(r, carry):
-            row_copy(d, r).wait_recv()
-            return carry
-
-        return lax.fori_loop(1, at.side, wait_row, carry)
-
-    lax.fori_loop(0, at.planes, wait_plane, 0)
-
-    lanes = recv[:, 2 * width :]
-    rows_p = from_parts(lanes)
-    for k in range(1, top_count):
-        rows_p = rows_p + from_parts(lanes, 3 * k)
-    step = min(512, width)
-    for c in range(width // step):
-        columns = pl.ds(c * step, step)
-        rows_g = recv[:, pl.ds(width + c * step, step)].astype(F32)
-        scaled[:, columns] = (rows_p * rows_g).astype(BF16)
-    span = min(256, half_width)
-
-    def through(n, carry):
-        gate_at = pl.multiple_of(n * span, span)
-        up_at = pl.multiple_of(half_width + n * span, span)
-        down_at = pl.multiple_of(wide + n * span, span)
-        gate_part = dot(recv[:, :width], full_ref[:, pl.ds(gate_at, span)])
-        up_part = dot(recv[:, :width], full_ref[:, pl.ds(up_at, span)])
-        hidden_grad = dot(scaled[...], full_ref[:, pl.ds(down_at, span)])
-        sigmoid = jax.nn.sigmoid(gate_part)
-        activated = gate_part * sigmoid
-        slope_term = sigmoid * (1.0 + gate_part * (1.0 - sigmoid))
-        hidden[:, pl.ds(gate_at, span)] = (activated * up_part).astype(BF16)
-        pre[:, pl.ds(gate_at, span)] = (hidden_grad * up_part * slope_term).astype(BF16)
-        pre[:, pl.ds(up_at, span)] = (hidden_grad * activated).astype(BF16)
-        return carry
-
-    lax.fori_loop(0, half_width // span, through, 0)
-
-    def weight_grads(i, carry):
-        start = pl.multiple_of(at.shard(i % 2, 2 + i // 2) * depth, depth)
-        columns = pl.ds(start, depth)
-        grad[i, :, pl.ds(0, wide)] = dot(recv[:, columns], pre[...], (0, 0)).astype(BF16)
-        grad[i, :, pl.ds(wide, half_width)] = dot(
-            scaled[:, columns], hidden[...], (0, 0)
-        ).astype(BF16)
-        return carry
+    for d in (0, 1, 3):
+        take_rows(d)
+    gathered(0)
+    take_rows(2)
 
     ring = (ring_send, ring_recv)
     summing = []
-    part = depth // SUM_CHUNKS
+    part = depth // HALVES
 
     def begin(source, target, kind, c, device):
         copy = send(source, target.at[c], ring, (kind, c), device)
@@ -413,39 +414,82 @@
         send(target.at[c], target.at[c], ring, (kind, c), at.up).wait_recv()
         return target[c].astype(F32)
 
-    def rows_of(c):
-        return pl.ds(c * part, part)
+    def piece_of(i, c):
+        return grad.at[c // HALVES, i, pl.ds((c % HALVES) * part, part)]
 
     A2, B2, A3, B3, A0, B0, A1, B1 = range(8)
     ON_UP, ON_DOWN, A_LOW, A_HIGH, B_LOW, B_HIGH, Z = range(7)
-    lax.fori_loop(0, 2, weight_grads, 0)
-    for c in range(SUM_CHUNKS):
-        begin(grad.at[A2, rows_of(c)], on_up, ON_UP, c, at.up)
-        begin(grad.at[B2, rows_of(c)], on_down, ON_DOWN, c, at.down)
-    lax.fori_loop(2, 8, weight_grads, 0)
-    early = SUM_CHUNKS // 2
-    for c in range(early):
-        begin(grad.at[B1, rows_of(c)], b_low, B_LOW, c, at.up)
-        begin(grad.at[A3, rows_of(c)], a_high, A_HIGH, c, at.down)
+
+    def through(n):
+        gate_part = dot(recv[:, :width], full_ref[n, :, pl.ds(0, span)])
+        up_part = dot(recv[:, :width], full_ref[n, :, pl.ds(span, span)])
+        hidden_grad = dot(scaled[...], full_ref[n, :, pl.ds(2 * span, span)])
+        sigmoid = jax.nn.sigmoid(gate_part)
+        activated = gate_part * sigmoid
+        slope_term = sigmoid * (1.0 + gate_part * (1.0 - sigmoid))
+        hidden[n] = (activated * up_part).astype(BF16)
+        pre[n, :, pl.ds(0, span)] = (hidden_grad * up_part * slope_term).astype(BF16)
+        pre[n, :, pl.ds(span, span)] = (hidden_grad * activated).astype(BF16)
+
+    def sum_up(n):
+        def weight_grads(i, carry):
+            start = pl.multiple_of(at.shard(i % 2, 2 + i // 2) * depth, depth)
+            rows = pl.ds(start, depth)
+            grad[n, i, :, pl.ds(0, 2 * span)] = dot(x_turned[rows], pre[n]).astype(BF16)
+            grad[n, i, :, pl.ds(2 * span, span)] = dot(s_turned[rows], hidden[n]).astype(BF16)
+            return carry
+
+        pieces_here = range(n * HALVES, (n + 1) * HALVES)
+        lax.fori_loop(0, 2, weight_grads, 0)
+        for c in pieces_here:
+            begin(piece_of(A2, c), on_up, ON_UP, c, at.up)
+            begin(piece_of(B2, c), on_down, ON_DOWN, c, at.down)
+        lax.fori_loop(2, 8, weight_grads, 0)
+        for c in pieces_here:
+            begin(piece_of(B1, c), b_low, B_LOW, c, at.up)
+            begin(piece_of(A3, c), a_high, A_HIGH, c, at.down)
+
+    for n in every:
+        if n > 0:
+            gathered(n)
+        through(n)
+        if n == 0:
+            sum_up(n)
+
+    def wait_sent(d, carry):
+        def wait_row(r, carry):
+            row_copy(d, r).wait_send()
+            return carry
+
+        return lax.fori_loop(1, at.side, wait_row, carry)
+
+    lax.fori_loop(0, at.planes, wait_sent, 0)
 
     span_out = min(256, width)
 
-    def row_grads(n, total):
-        start = pl.multiple_of(n * span_out, span_out)
+    ret = send_ref
+
+    def row_grads(i, total):
+        start = pl.multiple_of(i * span_out, span_out)
         rows = pl.ds(start, span_out)
-        ret[:, rows] = dot(pre[...], full_ref[rows, pl.ds(0, wide)], (1, 1)).astype(BF16)
-        out = dot(hidden[...], full_ref[rows, pl.ds(wide, half_width)], (1, 1)).astype(BF16)
+        row_grad = jnp.zeros((room, span_out), F32)
+        out = jnp.zeros((room, span_out), F32)
+        for n in every:
+            row_grad = row_grad + dot(pre[n], full_ref[n, rows, pl.ds(0, 2 * span)], (1, 1))
+            out = out + dot(hidden[n], full_ref[n, rows, pl.ds(2 * span, span)], (1, 1))
+        ret[:, rows] = row_grad.astype(BF16)
         rows_g = recv[:, pl.ds(pl.multiple_of(width + start, span_out), span_out)].astype(F32)
-        return total + jnp.sum(out.astype(F32) * rows_g, axis=1, keepdims=True)
+        return total + jnp.sum(out.astype(BF16).astype(F32) * rows_g, axis=1, keepdims=True)
 
     row_total = lax.fori_loop(0, width // span_out, row_grads, jnp.zeros((room, 1), F32))
-    ret[:, width:] = in_lanes(in_parts(row_total))
+    ret[:, pl.ds(width, LANES)] = in_lanes(in_parts(row_total))
 
     def rows_to(i):
         k = at.offset(i)
         rows = pl.ds(pl.multiple_of(k * capacity, capacity), capacity)
         device = at.member(at.side - k % at.side, at.planes - k // at.side)
-        return send(ret.at[rows], back.at[rows], (back_send, back_recv), k, device)
+        source = ret.at[rows, pl.ds(0, width + LANES)]
+        return send(source, back.at[rows], (back_send, back_recv), k, device)
 
     def start_rows(i, carry):
         rows_to(i).start()
@@ -456,53 +500,51 @@
         return carry
 
     lax.fori_loop(1, experts, start_rows, 0)
-    back[0:capacity] = ret[0:capacity]
+    for copy in moments[2:]:
+        copy.start()
+    back[0:capacity] = ret[0:capacity, pl.ds(0, width + LANES)]
+
+    for n in every[1:]:
+        sum_up(n)
 
     def pass_on(c):
-        low = grad[A1, rows_of(c)].astype(F32) + arrived(on_up, ON_UP, c)
-        grad[A1, rows_of(c)] = low.astype(BF16)
-        begin(grad.at[A1, rows_of(c)], a_low, A_LOW, c, at.up)
-        high = grad[B3, rows_of(c)].astype(F32) + arrived(on_down, ON_DOWN, c)
-        grad[B3, rows_of(c)] = high.astype(BF16)
-        begin(grad.at[B3, rows_of(c)], b_high, B_HIGH, c, at.down)
-
-    for c in range(SUM_CHUNKS):
+        low, high = piece_of(A1, c), piece_of(B3, c)
+        low[...] = (low[...].astype(F32) + arrived(on_up, ON_UP, c)).astype(BF16)
+        begin(low, a_low, A_LOW, c, at.up)
+        high[...] = (high[...].astype(F32) + arrived(on_down, ON_DOWN, c)).astype(BF16)
+        begin(high, b_high, B_HIGH, c, at.down)
+
+    def hand_over(c):
+        other = piece_of(B0, c)
+        mine = other[...].astype(F32) + arrived(b_low, B_LOW, c) + arrived(b_high, B_HIGH, c)
+        other[...] = mine.astype(BF16)
+        begin(other, z_in, Z, c, at.across)
+
+    def add_up(c):
+        mine = piece_of(A0, c)[...].astype(F32)
+        mine = mine + arrived(a_low, A_LOW, c) + arrived(a_high, A_HIGH, c)
+        mine = mine + arrived(z_in, Z, c)
+        rows = pl.ds((c % HALVES) * part, part)
+        for n in range(3):
+            columns = pl.ds(n * half_width + c // HALVES * span, span)
+            total_ref[rows, columns] = mine[:, n * span : (n + 1) * span]
+
+    count = parts * HALVES
+    for c in range(count):
         pass_on(c)
-        if c + early < SUM_CHUNKS:
-            begin(grad.at[B1, rows_of(c + early)], b_low, B_LOW, c + early, at.up)
-            begin(grad.at[A3, rows_of(c + early)], a_high, A_HIGH, c + early, at.down)
-
-    def hand_over(c):
-        mine = grad[B0, rows_of(c)].astype(F32)
-        mine = mine + arrived(b_low, B_LOW, c) + arrived(b_high, B_HIGH, c)
-        grad[B0, rows_of(c)] = mine.astype(BF16)
-        begin(grad.at[B0, rows_of(c)], z_in, Z, c, at.across)
-
-    def add_up(c):
-        mine = grad[A0, rows_of(c)].astype(F32)
-        mine = mine + arrived(a_low, A_LOW, c) + arrived(a_high, A_HIGH, c)
-        total_ref[rows_of(c)] = mine + arrived(z_in, Z, c)
-
-    for c in range(SUM_CHUNKS):
+    for c in range(count):
         hand_over(c)
         if c > 0:
             add_up(c - 1)
-    add_up(SUM_CHUNKS - 1)
+    add_up(count - 1)
     lax.fori_loop(1, experts, wait_rows, 0)
     for copy in moments:
         copy.wait()
 
-    def wait_sent(d, carry):
-        def wait_row(r, carry):
-            row_copy(d, r).wait_send()
-            return carry
-
-        return lax.fori_loop(1, at.side, wait_row, carry)
-
-    lax.fori_loop(0, at.planes, wait_sent, 0)
     for kind in range(3):
         for h in range(2):
-            to_plane(kind, h).wait_send()
+            for piece in range(3):
+                to_plane(kind, h, piece).wait_send()
     for pair in swaps:
         for copy in pair:
             copy.wait_send()
@@ -529,7 +571,8 @@
         weight = weight_ref[:, columns].astype(F32)
         first_new = beta_one * first + (1.0 - beta_one) * value
         second_new = beta_two * second + (1.0 - beta_two) * value * value
-        step_size = first_new / bias_one / (jnp.sqrt(second_new / bias_two) + adam_eps)
+        root = jnp.sqrt(second_new * (1.0 / bias_two)) + adam_eps
+        step_size = first_new * (1.0 / bias_one) / root
         refs[4][...] = (weight - learn_rate * step_size).astype(BF16)
         refs[5][...] = first_new.astype(BF16)
         refs[6][...] = second_new.astype(BF16)
@@ -542,7 +585,7 @@
     @pl.when(pl.program_id(0) == 0)
     def _():
         for k, hot in enumerate(hots):
-            prob_ref[:, k : k + 1] = from_parts(dot(hot, back_lanes[...]))
+            prob_ref[k : k + 1, :] = row_of(from_parts(dot(hot, back_lanes[...])))
 
 
 def body(
@@ -575,7 +618,10 @@
     anywhere = pl.BlockSpec(memory_space=pl.ANY)
     dma = pltpu.SemaphoreType.DMA
     shape = jax.ShapeDtypeStruct
-    chunked = pltpu.VMEM((SUM_CHUNKS, depth // SUM_CHUNKS, joint), BF16)
+    span = min(PART_UNITS, half_width)
+    parts = half_width // span
+    pieces = parts * HALVES
+    chunked = pltpu.VMEM((pieces, depth // HALVES, 3 * span), BF16)
     state_in, state_down = shape((depth, wide), BF16), shape((depth, half_width), BF16)
     moments = (m_in[0], m_down[0], v_in[0], v_down[0])
     total, weight, back, hots, *moved = pl.pallas_call(
@@ -594,22 +640,23 @@
             pltpu.VMEM((planes, tok_rows, row_width), BF16),
             pltpu.VMEM((room, row_width), BF16),
             pltpu.VMEM((room, row_width), BF16),
-            pltpu.VMEM((dp * depth, joint), BF16),
+            pltpu.VMEM((parts, dp * depth, 3 * span), BF16),
             pltpu.VMEM((depth, wide), BF16),
             pltpu.VMEM((depth, half_width), BF16),
             pltpu.VMEM((room, width), BF16),
-            pltpu.VMEM((room, wide), BF16),
-            pltpu.VMEM((room, half_width), BF16),
-            pltpu.VMEM((dp, depth, joint), BF16),
-            pltpu.VMEM((room, width + LANES), BF16),
+            pltpu.VMEM((width, room), BF16),
+            pltpu.VMEM((width, room), BF16),
+            pltpu.VMEM((parts, room, 2 * span), BF16),
+            pltpu.VMEM((parts, room, span), BF16),
+            pltpu.VMEM((parts, dp, depth, 3 * span), BF16),
         ]
         + [chunked] * 7
-        + [dma((3, 2))] * 2
+        + [dma((3, 2, 3))] * 2
         + [dma((experts,))] * 4
-        + [dma((2, GATHER_CHUNKS))] * 2
+        + [dma((3, parts))] * 2
         + [dma((4,))] * 2
-        + [dma((7, GATHER_CHUNKS))] * 2
-        + [dma((7, SUM_CHUNKS))] * 2,
+        + [dma((7, parts))] * 2
+        + [dma((7, pieces))] * 2,
         compiler_params=pltpu.CompilerParams(
             collective_id=0, has_side_effects=True, vmem_limit_bytes=VMEM_BYTES
         ),
@@ -634,7 +681,7 @@
         update_kernel,
         name="update",
         grid=(steps,),
-        out_shape=(shape((tok_rows, width), BF16), shape((tok_rows, top_count), F32))
+        out_shape=(shape((tok_rows, width), BF16), shape((top_count, tok_rows), F32))
         + (state_in, state_down) * 3,
         in_specs=[
             smem,
@@ -647,11 +694,11 @@
         + states * 4,
         out_specs=[
             pl.BlockSpec((tok_rows, width // steps), lambda i: (0, i)),
-            pl.BlockSpec((tok_rows, top_count), lambda i: (0, 0)),
+            pl.BlockSpec((top_count, tok_rows), lambda i: (0, 0)),
         ]
         + states * 3,
     )(swap_pairs, total, weight, back, back, hots, *moments, *moved)
-    return tuple(result[:2]) + tuple(r[None] for r in result[2:])
+    return (result[0], result[1].T) + tuple(r[None] for r in result[2:])
 
 
 def solution(mesh):

time: 243 us -> 235 us (0.967)
  Pallas kernels: 241 us -> 234 us
    pallas_call x1, Pallas kernels: 232 us -> 225 us  [body(): pl.pallas_call(layer_kernel, name='layer', out_shape=(shape((depth, joint...]
where the time goes in v3:
time: 235 us
  Pallas kernels  234 us (100%)
    pallas_call x1, Pallas kernels, body(): pl.pallas_call(layer_kernel, name='layer', out_shape=(shape((depth, joint...  225 us
    pallas_call x1, Pallas kernels, body(): pl.pallas_call(update_kernel, name='update', grid=(steps,), out_shape=(sh...  8.86 us

profile of v3, /device:TPU:33, one launch (start us, length us, event | category | flops | bytes accessed | tf_op | source)
XLA Modules:
  0.0 235.0 jit_solution(16764564377179818804)
XLA Ops:
  0.6 225.3 %layer.1 = (f32[256,2304]{1,0:T(8,128)}, bf16[256,2304]{1,0:T(8,128)(2,1)}, bf16[512,2176]{1,0:T(8,128)(2,1)}, bf16[2,128,512]{2,1,0:T(8,128)(2,1)}, bf16[256,15...) custom-call(s32[2,128]{1,0:T(2,128)} %bitcast.26, ...), custom_call_target="tpu_custom_call" | custom-call | tf_op jit(solution)/shard_map/layer/pallas_call | solution.py:627
  226.0 8.9 %update.1 = (bf16[128,2048]{1,0:T(8,128)(2,1)}, f32[2,128]{1,0:T(2,128)}, bf16[256,1536]{1,0:T(8,128)(2,1)}, bf16[256,768]{1,0:T(8,128)(2,1)}, bf16[256,1536]{1,...) custom-call(s32[4]{0:T(128)} %pairs_ref.3, ...), custom_call_target="tpu_custom_call" | custom-call | tf_op jit(solution)/shard_map/update/pallas_call | solution.py:680

commit v4 on v3

--- a/solution.py
+++ b/solution.py
@@ -23,7 +23,7 @@
 
 LANES = 128
 PART_UNITS = 256
-HALVES = 2
+HALVES = 4
 ADAM_STEPS = 4
 VMEM_BYTES = 60 * 1024 * 1024
 

time: 235 us -> 236 us (level)
  no operation moved by 1% of the time
where the time goes in v4:
time: 236 us; the launch traced here: 234 us
  Pallas kernels  233 us (99%)
    pallas_call x1, Pallas kernels, body(): pl.pallas_call(layer_kernel, name='layer', out_shape=(shape((depth, joint...  224 us
    pallas_call x1, Pallas kernels, body(): pl.pallas_call(update_kernel, name='update', grid=(steps,), out_shape=(sh...  8.86 us

profile of v4, /device:TPU:33, one launch (start us, length us, event | category | flops | bytes accessed | tf_op | source)
XLA Modules:
  0.0 233.7 jit_solution(13052467164884085549)
XLA Ops:
  0.6 224.1 %layer.1 = (f32[256,2304]{1,0:T(8,128)}, bf16[256,2304]{1,0:T(8,128)(2,1)}, bf16[512,2176]{1,0:T(8,128)(2,1)}, bf16[2,128,512]{2,1,0:T(8,128)(2,1)}, bf16[256,15...) custom-call(s32[2,128]{1,0:T(2,128)} %bitcast.26, ...), custom_call_target="tpu_custom_call" | custom-call | tf_op jit(solution)/shard_map/layer/pallas_call | solution.py:627
  224.7 8.9 %update.1 = (bf16[128,2048]{1,0:T(8,128)(2,1)}, f32[2,128]{1,0:T(2,128)}, bf16[256,1536]{1,0:T(8,128)(2,1)}, bf16[256,768]{1,0:T(8,128)(2,1)}, bf16[256,1536]{1,...) custom-call(s32[4]{0:T(128)} %pairs_ref.3, ...), custom_call_target="tpu_custom_call" | custom-call | tf_op jit(solution)/shard_map/update/pallas_call | solution.py:680
